TPU v7x, 32 devices: a whole 2x2x4 slice. The times are simulated.
32 devices in a mesh: grp: 8 (over z, x), sp: 4 (over y, core).
Axes of the slice: x: 2, y: 2, z: 4, core: 2. Of those that a mesh axis runs over, the one named last changes fastest.
Arguments:
- query_rows: bfloat16 [4096, 4096], P(('grp', 'sp')), parts along dimension 0, may hold values from -250 to 250
- key_rows: bfloat16 [4096, 1024], P(('grp', 'sp')), parts along dimension 0, may hold values from -4 to 4
- value_rows: bfloat16 [4096, 1024], P(('grp', 'sp')), parts along dimension 0, may hold values from -6 to 6
- out_grad: bfloat16 [4096, 4096], P(('grp', 'sp')), parts along dimension 0, may hold values from -6 to 6
- question_lengths: int32 [64], P('grp'), parts along dimension 0, may hold values from 1 to 128, 256 in all
Outputs:
- query_grad: bfloat16 [4096, 4096], P(('grp', 'sp')), parts along dimension 0
- key_grad: bfloat16 [4096, 1024], P(('grp', 'sp')), parts along dimension 0
- value_grad: bfloat16 [4096, 1024], P(('grp', 'sp')), parts along dimension 0
There are 8 independent parts, one for each index of `grp`. A program takes and returns all parts, laid end to end along the dimension named above; each array names one. Nothing has to cross between parts.
All inputs are finite; a program needn't handle non-finite values.
Results may differ from a plain program's by a relative error of at most 0.033.
Values may be sent and summed in bfloat16 or wider, within the bound.
No kernel may reach another device: no remote copies, remote signals or barrier semaphores. Data moves between devices by JAX's collectives and lax.ppermute only.
A program may use at most 128 MiB of HBM per device.

v0:
```python
from functools import partial
from functools import reduce
import math

import jax
import jax.numpy as jnp
from jax import lax
from jax.sharding import PartitionSpec as P

HD = 128
QH = 32
KVH = 8


MASKED = -1e30


def widen(rows, copies):
    tokens = rows.shape[0]
    shaped = rows.reshape(tokens, KVH, 1, HD)
    return jnp.broadcast_to(shaped, (tokens, KVH, copies, HD)).reshape(tokens, KVH * copies * HD)


def segment_ids(question_lengths, length, doc_len):
    ends = jnp.cumsum(question_lengths)
    places = jnp.arange(length, dtype=jnp.int32)
    inside = jnp.sum((ends[None, :] <= (places - doc_len)[:, None]).astype(jnp.int32), axis=1)
    return jnp.where(places < doc_len, -1, inside)


def make_scores(query_block, key_block, visible, scaling):
    raw = (
        jnp.einsum("bkgd,skd->kgbs", query_block, key_block, preferred_element_type=jnp.float32)
        * scaling
    )
    return jnp.where(visible[None, None], raw, MASKED)


def weighted_values(probs_b, value_block):
    return jnp.einsum("kgbs,skd->bkgd", probs_b, value_block, preferred_element_type=jnp.float32)


def backward_block(probs, probs_b, delta, grad_block, query_block, key_block, value_block, scaling):
    value_part = jnp.einsum(
        "kgbs,bkgd->skd", probs_b, grad_block, preferred_element_type=jnp.float32
    )
    prob_grad = jnp.einsum(
        "bkgd,skd->kgbs", grad_block, value_block, preferred_element_type=jnp.float32
    )
    score_grad = (probs * (prob_grad - delta[..., None])).astype(jnp.bfloat16)
    query_part = jnp.einsum(
        "kgbs,skd->bkgd", score_grad, key_block, preferred_element_type=jnp.float32
    )
    key_part = (
        jnp.einsum("kgbs,bkgd->skd", score_grad, query_block, preferred_element_type=jnp.float32)
        * scaling
    )
    return (query_part, key_part, value_part)


def on_device(query_rows, key_rows, value_rows, out_grad, question_lengths):
    devices = lax.axis_size("sp")
    tokens = query_rows.shape[0]
    length = tokens * devices
    doc_len = length // 2
    block_len = min(512, length)
    block_count = length // block_len
    scaling = 1.0 / math.sqrt(HD)
    copies = max(KVH, devices) // KVH
    keys_local, values_local = (
        lax.all_to_all(widen(key_rows, copies), "sp", split_axis=1, concat_axis=0, tiled=True),
        lax.all_to_all(widen(value_rows, copies), "sp", split_axis=1, concat_axis=0, tiled=True),
    )
    queries_local, grads_local = (
        lax.all_to_all(query_rows, "sp", split_axis=1, concat_axis=0, tiled=True),
        lax.all_to_all(out_grad, "sp", split_axis=1, concat_axis=0, tiled=True),
    )
    key_heads = KVH * copies // devices
    per_group = QH // devices // key_heads
    queries = queries_local.reshape(length, key_heads, per_group, HD)
    grads = grads_local.reshape(length, key_heads, per_group, HD)
    keys = keys_local.reshape(length, key_heads, HD)
    values = values_local.reshape(length, key_heads, HD)
    segment = segment_ids(question_lengths, length, doc_len)
    places = jnp.arange(length, dtype=jnp.int32)
    query_shape = (block_len, key_heads, per_group, HD)
    key_shape = (block_len, key_heads, HD)
    key_sums = [jnp.zeros(key_shape, jnp.float32)] * block_count
    value_sums = [jnp.zeros(key_shape, jnp.float32)] * block_count
    query_parts = []
    for row_block in range(block_count):
        row_start = row_block * block_len
        query_block = queries[row_start : row_start + block_len]
        grad_block = grads[row_start : row_start + block_len]
        row_places = places[row_start : row_start + block_len]
        row_segment = segment[row_start : row_start + block_len]
        needs = []
        scores = []
        for col_block in range(row_block + 1):
            col_start = col_block * block_len
            col_places = places[col_start : col_start + block_len]
            col_segment = segment[col_start : col_start + block_len]
            visible = (col_places[None, :] <= row_places[:, None]) & (
                (col_places[None, :] < doc_len) | (col_segment[None, :] == row_segment[:, None])
            )
            needed = True
            needs.append(needed)
            scores.append(
                make_scores(query_block, keys[col_start : col_start + block_len], visible, scaling)
            )
        peak = reduce(jnp.maximum, [jnp.max(score, axis=3) for score in scores])
        total = reduce(
            jnp.add, [jnp.sum(jnp.exp(score - peak[..., None]), axis=3) for score in scores]
        )
        log_total = peak + jnp.log(total)
        probs = [jnp.exp(score - log_total[..., None]) for score in scores]
        probs_low = [single.astype(jnp.bfloat16) for single in probs]
        output = jnp.zeros(query_shape, jnp.float32)
        for col_block in range(row_block + 1):
            col_start = col_block * block_len
            output = output + weighted_values(
                probs_low[col_block], values[col_start : col_start + block_len]
            )
        output_low = output.astype(jnp.bfloat16)
        delta = jnp.einsum(
            "bkgd,bkgd->kgb", grad_block, output_low, preferred_element_type=jnp.float32
        )
        query_sum = jnp.zeros(query_shape, jnp.float32)
        for col_block in range(row_block + 1):
            col_start = col_block * block_len
            action = partial(
                backward_block,
                probs[col_block],
                probs_low[col_block],
                delta,
                grad_block,
                query_block,
                keys[col_start : col_start + block_len],
                values[col_start : col_start + block_len],
                scaling,
            )
            query_part, key_part, value_part = action()
            query_sum = query_sum + query_part
            key_sums[col_block] = key_sums[col_block] + key_part
            value_sums[col_block] = value_sums[col_block] + value_part
        query_parts.append((query_sum * scaling).astype(jnp.bfloat16))
    query_local = jnp.concatenate(query_parts, axis=0).reshape(length, key_heads * per_group * HD)
    key_local = jnp.concatenate(key_sums, axis=0).reshape(length, key_heads * HD)
    value_local = jnp.concatenate(value_sums, axis=0).reshape(length, key_heads * HD)
    query_grad = lax.all_to_all(query_local, "sp", split_axis=0, concat_axis=1, tiled=True)
    key_back, value_back = (
        lax.all_to_all(key_local, "sp", split_axis=0, concat_axis=1, tiled=True),
        lax.all_to_all(value_local, "sp", split_axis=0, concat_axis=1, tiled=True),
    )
    key_grad = (
        jnp.sum(key_back.reshape(tokens, KVH, copies, HD), axis=2)
        .reshape(tokens, KVH * HD)
        .astype(jnp.bfloat16)
    )
    value_grad = (
        jnp.sum(value_back.reshape(tokens, KVH, copies, HD), axis=2)
        .reshape(tokens, KVH * HD)
        .astype(jnp.bfloat16)
    )
    return (query_grad, key_grad, value_grad)


def solution(mesh):
    return jax.shard_map(
        on_device,
        mesh=mesh,
        in_specs=(
            P(("grp", "sp"), None),
            P(("grp", "sp"), None),
            P(("grp", "sp"), None),
            P(("grp", "sp"), None),
            P("grp"),
        ),
        out_specs=(P(("grp", "sp"), None), P(("grp", "sp"), None), P(("grp", "sp"), None)),
        check_vma=False,
    )
```

profile of v0, /device:TPU:0, one launch (start us, length us, event | category | flops | bytes accessed | tf_op | source)
XLA Modules:
  0.0 117.2 jit_solution(11566615232329075632)
XLA Ops:
  0.6 1.7 %copy.125 = bf16[16,4,8,256]{3,2,0,1:T(8,128)(2,1)} copy(bf16[16,4,8,256]{3,2,1,0:T(8,128)(2,1)} %bitcast.94) | data formatting | bytes 524288 | tf_op jit(solution)/shard_map/all_to_all | solution.py:71
  2.3 4.3 %all-to-all-start = ((bf16[128,4,256]{2,0,1:T(8,128)(2,1)}), bf16[128,4,256]{2,0,1:T(8,128)(2,1)S(1)}, u32[]{:S(2)}, u32[]{:S(2)}) async-start(bf16[128,4,256]{2,0,1:T(8,128)(2,1)} %bitcast.76), calls=%async_computation | async-start | bytes 524288 | tf_op jit(solution)/shard_map/all_to_all | solution.py:71
  6.6 1.7 %copy.124 = bf16[16,4,8,256]{3,2,0,1:T(8,128)(2,1)} copy(bf16[16,4,8,256]{3,2,1,0:T(8,128)(2,1)} %bitcast.95) | data formatting | bytes 524288 | tf_op jit(solution)/shard_map/all_to_all | solution.py:72
  8.2 4.3 %all-to-all-done = bf16[128,4,256]{2,0,1:T(8,128)(2,1)S(1)} async-done(((bf16[128,4,256]{2,0,1:T(8,128)(2,1)}), bf16[128,4,256]{2,0,1:T(8,128)(2,1)S(1)}, u32[]{:S(2)}, u32[]{:S(2)}) %all-to-all-start) | async-done | bytes 262176 | tf_op jit(solution)/shard_map/all_to_all | solution.py:71
  12.6 3.4 %all-to-all-start.2 = ((bf16[128,4,256]{2,0,1:T(8,128)(2,1)}), bf16[128,4,256]{2,0,1:T(8,128)(2,1)S(1)}, u32[]{:S(2)}, u32[]{:S(2)}) async-start(bf16[128,4,256]{2,0,1:T(8,128)(2,1)} %bitcast.75), calls=%async_computation.2 | async-start | bytes 524288 | tf_op jit(solution)/shard_map/all_to_all | solution.py:72
  16.0 2.3 %copy.123 = bf16[16,4,8,1024]{3,2,0,1:T(8,128)(2,1)} copy(bf16[16,4,8,1024]{3,2,1,0:T(8,128)(2,1)} %bitcast.84) | data formatting | bytes 2097152 | tf_op jit(solution)/shard_map/all_to_all | solution.py:75
  18.3 3.7 %all-to-all-done.2 = bf16[128,4,256]{2,0,1:T(8,128)(2,1)S(1)} async-done(((bf16[128,4,256]{2,0,1:T(8,128)(2,1)}), bf16[128,4,256]{2,0,1:T(8,128)(2,1)S(1)}, u32[]{:S(2)}, u32[]{:S(2)}) %all-to-all-start.2) | async-done | bytes 262176 | tf_op jit(solution)/shard_map/all_to_all | solution.py:72
  22.0 3.5 %all-to-all-start.1 = ((bf16[128,4,1024]{2,0,1:T(8,128)(2,1)}), bf16[128,4,1024]{2,0,1:T(8,128)(2,1)S(1)}, u32[]{:S(2)}, u32[]{:S(2)}) async-start(bf16[128,4,1024]{2,0,1:T(8,128)(2,1)} %bitcast.74), calls=%async_computation.1 | async-start | bytes 2097152 | tf_op jit(solution)/shard_map/all_to_all | solution.py:75
  25.5 2.3 %copy.122 = bf16[16,4,8,1024]{3,2,0,1:T(8,128)(2,1)} copy(bf16[16,4,8,1024]{3,2,1,0:T(8,128)(2,1)} %bitcast.85) | data formatting | bytes 2097152 | tf_op jit(solution)/shard_map/all_to_all | solution.py:76
  28.0 11.9 %all-to-all-done.1 = bf16[128,4,1024]{2,0,1:T(8,128)(2,1)S(1)} async-done(((bf16[128,4,1024]{2,0,1:T(8,128)(2,1)}), bf16[128,4,1024]{2,0,1:T(8,128)(2,1)S(1)}, u32[]{:S(2)}, u32[]{:S(2)}) %all-to-all-start.1) | async-done | bytes 1048608 | tf_op jit(solution)/shard_map/all_to_all | solution.py:75
  39.9 3.5 %all-to-all-start.3 = ((bf16[128,4,1024]{2,0,1:T(8,128)(2,1)}), bf16[128,4,1024]{2,0,1:T(8,128)(2,1)S(1)}, u32[]{:S(2)}, u32[]{:S(2)}) async-start(bf16[128,4,1024]{2,0,1:T(8,128)(2,1)} %bitcast.73), calls=%async_computation.3 | async-start | bytes 2097152 | tf_op jit(solution)/shard_map/all_to_all | solution.py:76
  46.1 11.8 %all-to-all-done.3 = bf16[128,4,1024]{2,0,1:T(8,128)(2,1)S(1)} async-done(((bf16[128,4,1024]{2,0,1:T(8,128)(2,1)}), bf16[128,4,1024]{2,0,1:T(8,128)(2,1)S(1)}, u32[]{:S(2)}, u32[]{:S(2)}) %all-to-all-start.3) | async-done | bytes 1048608 | tf_op jit(solution)/shard_map/all_to_all | solution.py:76
  58.6 2.6 %fusion.3 = (f32[2,4,512]{2,1,0:T(4,128)S(1)}, f32[2,512,512,4]{2,1,3,0:T(8,128)S(1)}) fusion(pred[512,512]{0,1:T(8,128)(4,1)S(1)} %fusion.8, bf16[512,2,4,128]{3,2,1,0:T(4,128)(2,1)S(1)} %reshape.174, bf16[512,2,128,1]{2,1,0,3:T(2,128)(2,1)} %bitcast.92), kind=kOutput, calls=%fused_computation.7 | convolution fusion | flops 543158272 | bytes 9977856 | tf_op jit(solution)/shard_map/bkgd,skd->kgbs/dot_general | solution.py:33
  61.2 1.8 %exponential_reduce_fusion = f32[2,4,512]{2,1,0:T(4,128)S(1)} fusion(f32[2,512,512,4]{2,1,3,0:T(8,128)S(1)} %get-tuple-element.10, f32[2,4,512]{2,1,0:T(4,128)S(1)} %get-tuple-element.9, pred[512,512]{0,1:T(8,128)(4,1)S(1)} %fusion.8), kind=kLoop, calls=%fused_computation.5 | loop fusion | flops 8384512 | bytes 8683520 | tf_op jit(solution)/shard_map/reduce_sum | solution.py:113
  63.0 2.1 %convolution_bitcast_fusion = bf16[512,2,128]{2,0,1:T(8,128)(2,1)S(1)} fusion(bf16[512,2,4,128]{3,2,1,0:T(4,128)(2,1)S(1)} %reshape.176, f32[2,512,512,4]{2,1,3,0:T(8,128)S(1)} %get-tuple-element.10, f32[2,4,512]{2,1,0:T(4,128)S(1)} %bitcast.100, pred[512,512]{0,1:T(8,128)(4,1)S(1)} %fusion.8), kind=kOutput, calls=%fused_computation.13 | convolution fusion | flops 545259520 | bytes 9977856 | tf_op jit(solution)/shard_map/kgbs,bkgd->skd/dot_general | solution.py:44
  66.3 3.6 %all-to-all-start.6 = ((bf16[4,128,256]{2,1,0:T(8,128)(2,1)}), bf16[4,128,256]{2,1,0:T(8,128)(2,1)S(1)}, u32[]{:S(2)}, u32[]{:S(2)}) async-start(bf16[4,128,256]{2,1,0:T(8,128)(2,1)} %all_to_all.100), calls=%async_computation.6 | async-start | bytes 524288 | tf_op jit(solution)/shard_map/all_to_all | solution.py:153
  69.9 5.9 %fusion.4 = f32[2,4,512,128]{3,2,1,0:T(8,128)S(1)} fusion(bf16[512,2,128,1]{2,1,0,3:T(2,128)(2,1)S(1)} %bitcast.96, f32[2,512,512,4]{2,1,3,0:T(8,128)} %copy-done, f32[2,4,512]{2,1,0:T(4,128)S(1)} %bitcast.101, pred[512,512]{0,1:T(8,128)(4,1)S(1)} %fusion.8), kind=kOutput, calls=%fused_computation.11 | convolution fusion | flops 546308096 | bytes 11026432 | tf_op jit(solution)/shard_map/kgbs,skd->bkgd/dot_general | solution.py:40
  75.8 2.1 %multiply_reduce_fusion = f32[2,4,512]{1,0,2:T(2,128)S(1)} fusion(f32[2,4,512,128]{3,2,1,0:T(8,128)S(1)} %fusion.4, bf16[512,2,4,128]{3,2,1,0:T(4,128)(2,1)S(1)} %reshape.176), kind=kLoop, calls=%fused_computation.8 | loop fusion | flops 1568768 | bytes 3162112
  78.1 5.1 %fusion.1 = bf16[2,4,512,512]{2,3,1,0:T(8,128)(2,1)S(1)} fusion(f32[2,512,512,4]{2,1,3,0:T(8,128)} %copy-done, f32[2,4,512]{2,1,0:T(4,128)S(1)} %copy.80, f32[2,4,512]{2,1,0:T(4,128)S(1)} %bitcast.102, pred[512,512]{0,1:T(8,128)(4,1)S(1)} %fusion.8, bf16[512,2,4,128]{3,2,1,0:T(4,128)(2,1)S(1)} %reshape.176, bf16[512,2,128,1]{2,1,0,3:T(2,128)(2,1)S(1)} %bitcast.97), kind=kOutput, calls=%fused_computation.2 | convolution fusion | flops 549453824 | bytes 14188544 | tf_op jit(solution)/shard_map/bkgd,skd->kgbs/dot_general | solution.py:47
  83.2 1.9 %copy-done.1 = bf16[2,4,512,512]{2,3,1,0:T(8,128)(2,1)} copy-done((bf16[2,4,512,512]{2,3,1,0:T(8,128)(2,1)}, bf16[2,4,512,512]{2,3,1,0:T(8,128)(2,1)S(1)}, u32[]{:S(2)}) %copy-start.1) | copy-done | bytes 4194328
  87.6 3.4 %all-to-all-start.5 = ((bf16[4,128,256]{2,1,0:T(8,128)(2,1)}), bf16[4,128,256]{2,1,0:T(8,128)(2,1)S(1)}, u32[]{:S(2)}, u32[]{:S(2)}) async-start(bf16[4,128,256]{2,1,0:T(8,128)(2,1)} %all_to_all.98), calls=%async_computation.5 | async-start | bytes 524288 | tf_op jit(solution)/shard_map/all_to_all | solution.py:152
  91.0 3.9 %fusion.5 = bf16[512,2,4,128]{3,0,2,1:T(8,128)(2,1)S(1)} fusion(bf16[2,4,512,512]{2,3,1,0:T(8,128)(2,1)} %copy-done.1, bf16[512,2,128,1]{2,1,0,3:T(2,128)(2,1)S(1)} %bitcast.93), kind=kOutput, calls=%fused_computation.12 | convolution fusion | flops 537919488 | bytes 5505024 | tf_op jit(solution)/shard_map/kgbs,skd->bkgd/dot_general | solution.py:51
  97.3 3.5 %all-to-all-start.4 = ((bf16[4,128,1024]{2,1,0:T(8,128)(2,1)}), bf16[4,128,1024]{2,1,0:T(8,128)(2,1)S(1)}, u32[]{:S(2)}, u32[]{:S(2)}) async-start(bf16[4,128,1024]{2,1,0:T(8,128)(2,1)} %all_to_all.94), calls=%async_computation.4 | async-start | bytes 2097152 | tf_op jit(solution)/shard_map/all_to_all | solution.py:150
  102.9 12.3 %all-to-all-done.4 = bf16[4,128,1024]{2,1,0:T(8,128)(2,1)S(1)} async-done(((bf16[4,128,1024]{2,1,0:T(8,128)(2,1)}), bf16[4,128,1024]{2,1,0:T(8,128)(2,1)S(1)}, u32[]{:S(2)}, u32[]{:S(2)}) %all-to-all-start.4) | async-done | bytes 1048608 | tf_op jit(solution)/shard_map/all_to_all | solution.py:150
  (36 shorter events, 13.7 us)
Async XLA Ops:
  0.6 27.2 %copy-start.4 = (s32[8]{0:T(128)S(1)}, s32[8]{0:T(128)}, u32[]{:S(2)}) copy-start(s32[8]{0:T(128)} %param.9) | copy-start | bytes 100
  2.3 10.3 %all-to-all-start = ((bf16[128,4,256]{2,0,1:T(8,128)(2,1)}), bf16[128,4,256]{2,0,1:T(8,128)(2,1)S(1)}, u32[]{:S(2)}, u32[]{:S(2)}) async-start(bf16[128,4,256]{2,0,1:T(8,128)(2,1)} %bitcast.76), calls=%async_computation | async-start | bytes 524288 | tf_op jit(solution)/shard_map/all_to_all | solution.py:71
  12.6 9.4 %all-to-all-start.2 = ((bf16[128,4,256]{2,0,1:T(8,128)(2,1)}), bf16[128,4,256]{2,0,1:T(8,128)(2,1)S(1)}, u32[]{:S(2)}, u32[]{:S(2)}) async-start(bf16[128,4,256]{2,0,1:T(8,128)(2,1)} %bitcast.75), calls=%async_computation.2 | async-start | bytes 524288 | tf_op jit(solution)/shard_map/all_to_all | solution.py:72
  22.0 17.9 %all-to-all-start.1 = ((bf16[128,4,1024]{2,0,1:T(8,128)(2,1)}), bf16[128,4,1024]{2,0,1:T(8,128)(2,1)S(1)}, u32[]{:S(2)}, u32[]{:S(2)}) async-start(bf16[128,4,1024]{2,0,1:T(8,128)(2,1)} %bitcast.74), calls=%async_computation.1 | async-start | bytes 2097152 | tf_op jit(solution)/shard_map/all_to_all | solution.py:75
  39.9 17.9 %all-to-all-start.3 = ((bf16[128,4,1024]{2,0,1:T(8,128)(2,1)}), bf16[128,4,1024]{2,0,1:T(8,128)(2,1)S(1)}, u32[]{:S(2)}, u32[]{:S(2)}) async-start(bf16[128,4,1024]{2,0,1:T(8,128)(2,1)} %bitcast.73), calls=%async_computation.3 | async-start | bytes 2097152 | tf_op jit(solution)/shard_map/all_to_all | solution.py:76
  61.2 3.9 %copy-start = (f32[2,512,512,4]{2,1,3,0:T(8,128)}, f32[2,512,512,4]{2,1,3,0:T(8,128)S(1)}, u32[]{:S(2)}) copy-start(f32[2,512,512,4]{2,1,3,0:T(8,128)S(1)} %get-tuple-element.10) | copy-start | bytes 25165828
  63.0 6.9 %copy-start.3 = (bf16[512,2,128]{2,1,0:T(2,128)(2,1)S(1)}, bf16[512,2,128]{2,1,0:T(2,128)(2,1)}, u32[]{:S(2)}) copy-start(bf16[512,2,128]{2,1,0:T(2,128)(2,1)} %reshape.175) | copy-start | bytes 786436
  66.3 21.3 %all-to-all-start.6 = ((bf16[4,128,256]{2,1,0:T(8,128)(2,1)}), bf16[4,128,256]{2,1,0:T(8,128)(2,1)S(1)}, u32[]{:S(2)}, u32[]{:S(2)}) async-start(bf16[4,128,256]{2,1,0:T(8,128)(2,1)} %all_to_all.100), calls=%async_computation.6 | async-start | bytes 524288 | tf_op jit(solution)/shard_map/all_to_all | solution.py:153
  78.1 12.9 %copy-start.2 = (bf16[512,2,128]{2,1,0:T(2,128)(2,1)S(1)}, bf16[512,2,128]{2,1,0:T(2,128)(2,1)}, u32[]{:S(2)}) copy-start(bf16[512,2,128]{2,1,0:T(2,128)(2,1)} %reshape.173) | copy-start | bytes 786436
  83.2 1.9 %copy-start.1 = (bf16[2,4,512,512]{2,3,1,0:T(8,128)(2,1)}, bf16[2,4,512,512]{2,3,1,0:T(8,128)(2,1)S(1)}, u32[]{:S(2)}) copy-start(bf16[2,4,512,512]{2,3,1,0:T(8,128)(2,1)S(1)} %fusion.1) | copy-start | bytes 12582916
  87.6 9.7 %all-to-all-start.5 = ((bf16[4,128,256]{2,1,0:T(8,128)(2,1)}), bf16[4,128,256]{2,1,0:T(8,128)(2,1)S(1)}, u32[]{:S(2)}, u32[]{:S(2)}) async-start(bf16[4,128,256]{2,1,0:T(8,128)(2,1)} %all_to_all.98), calls=%async_computation.5 | async-start | bytes 524288 | tf_op jit(solution)/shard_map/all_to_all | solution.py:152
  97.3 17.9 %all-to-all-start.4 = ((bf16[4,128,1024]{2,1,0:T(8,128)(2,1)}), bf16[4,128,1024]{2,1,0:T(8,128)(2,1)S(1)}, u32[]{:S(2)}, u32[]{:S(2)}) async-start(bf16[4,128,1024]{2,1,0:T(8,128)(2,1)} %all_to_all.94), calls=%async_computation.4 | async-start | bytes 2097152 | tf_op jit(solution)/shard_map/all_to_all | solution.py:150
where the time goes:
time: 118 us; the launch traced here: 117 us
  waiting for transfers between devices  44 us (37%)
  starting transfers between devices  25.2 us (21%)
  local copies, waits for them, and re-layouts  21.7 us (18%)
  matrix products  21 us (18%)
  other arithmetic  4.36 us (4%)
    all_to_all x1, waiting for transfers between devices, on_device(): lax.all_to_all(query_local, 'sp', split_axis=0, concat_axis=1, tiled=True)  12.3 us
    all_to_all x1, waiting for transfers between devices, on_device(): lax.all_to_all(query_rows, 'sp', split_axis=1, concat_axis=0, tiled=True)  11.9 us
    all_to_all x1, waiting for transfers between devices, on_device(): lax.all_to_all(out_grad, 'sp', split_axis=1, concat_axis=0, tiled=True)  11.8 us
    dot_general x1, matrix products, weighted_values(): jnp.einsum('kgbs,skd->bkgd', probs_b, value_block, preferred_element_type...  5.91 us
    dot_general x1, matrix products, backward_block(): jnp.einsum('bkgd,skd->kgbs', grad_block, value_block, preferred_element_t...  5.15 us
    unnamed x13, local copies, waits for them, and re-layouts  4.96 us
    all_to_all x1, waiting for transfers between devices, on_device(): lax.all_to_all(widen(key_rows, copies), 'sp', split_axis=1, concat_axis=0...  4.34 us
    all_to_all x1, starting transfers between devices, on_device(): lax.all_to_all(widen(key_rows, copies), 'sp', split_axis=1, concat_axis=0...  4.26 us
  transfers between devices with their start and end apart: 7, of which 5 were waited for; matrix products, arithmetic and copies ran while one was open for 26% of the time, Pallas kernels for 0%

commit v1 on v0

--- a/solution.py
+++ b/solution.py
@@ -5,11 +5,16 @@
 import jax
 import jax.numpy as jnp
 from jax import lax
+from jax.experimental import pallas as pl
+from jax.experimental.pallas import tpu as pltpu
 from jax.sharding import PartitionSpec as P
 
 HD = 128
 QH = 32
 KVH = 8
+
+LAG = 2
+VMEM_BYTES = 32 * 1024 * 1024
 
 
 MASKED = -1e30
@@ -94,7 +99,6 @@
         grad_block = grads[row_start : row_start + block_len]
         row_places = places[row_start : row_start + block_len]
         row_segment = segment[row_start : row_start + block_len]
-        needs = []
         scores = []
         for col_block in range(row_block + 1):
             col_start = col_block * block_len
@@ -103,8 +107,6 @@
             visible = (col_places[None, :] <= row_places[:, None]) & (
                 (col_places[None, :] < doc_len) | (col_segment[None, :] == row_segment[:, None])
             )
-            needed = True
-            needs.append(needed)
             scores.append(
                 make_scores(query_block, keys[col_start : col_start + block_len], visible, scaling)
             )
@@ -165,17 +167,424 @@
     return (query_grad, key_grad, value_grad)
 
 
+LOG2E = 1.4426950408889634
+HIDDEN = -1e30
+
+
+def contract(left, right, left_dim, right_dim):
+    return lax.dot_general(
+        left, right, (((left_dim,), (right_dim,)), ((), ())), preferred_element_type=jnp.float32
+    )
+
+
+def start_all(pairs, sems):
+    copies = [pltpu.make_async_copy(src, dst, sems.at[i]) for i, (src, dst) in enumerate(pairs)]
+    for copy in copies:
+        copy.start()
+    return copies
+
+
+def halves_into(sources, side, out):
+    pairs, at = [], 0
+    for source in sources:
+        half = source.shape[1] // 2
+        start = pl.multiple_of(side * half, HD)
+        pairs.append((source.at[:, pl.ds(start, half)], out.at[:, at : at + half]))
+        at += half
+    return pairs
+
+
+def pack_kernel(place, queries, grads, keys, values, *refs):
+    *sends, sib_send, sems = refs
+    core = place[0] % 2
+    half = keys.shape[1] // 2
+    pairs = []
+    for index, out in enumerate(sends):
+        chunk, side = index // 2, index % 2
+        base = (core if side == 0 else 1 - core) * half
+        start = pl.multiple_of(base + chunk * HD, HD)
+        pairs.append((keys.at[:, pl.ds(start, HD)], out.at[:, :HD]))
+        pairs.append((values.at[:, pl.ds(start, HD)], out.at[:, HD:]))
+    pairs += halves_into((queries, grads, keys, values), 1 - core, sib_send)
+    for copy in start_all(pairs, sems):
+        copy.wait()
+
+
+def stage_kernel(place, queries, grads, keys, values, lengths, own_all, bias, spans, sems):
+    core = place[0] % 2
+    asking = place[0] // 2
+    pairs = [(lengths, spans)] + halves_into((queries, grads, keys, values), core, own_all)
+    copies = start_all(pairs, sems)
+    copies[0].wait()
+    spots = lax.broadcasted_iota(jnp.int32, bias.shape, 1)
+    key_spots = lax.broadcasted_iota(jnp.int32, bias.shape, 0)
+    spot_row = lax.broadcasted_iota(jnp.int32, (1, bias.shape[1]), 1)
+    begin = jnp.zeros((1, bias.shape[1]), jnp.int32)
+    end = jnp.int32(0)
+    for question in range(lengths.shape[0]):
+        end = end + spans[question]
+        begin = begin + jnp.where(spot_row >= end, spans[question], 0)
+    begin = begin * asking
+    bias[...] = jnp.where((key_spots <= spots) & (key_spots >= begin), 0.0, HIDDEN)
+    for copy in copies[1:]:
+        copy.wait()
+
+
+def specialise(place, body):
+    core, asking = place[0] % 2, place[0] // 2
+    for first in (True, False):
+        for asks in (True, False):
+            @pl.when((core == (0 if first else 1)) & (asking == (1 if asks else 0)))
+            def _(first=first, asks=asks):
+                body(asks, (lambda own, sib: (own, sib)) if first else (lambda own, sib: (sib, own)))
+
+
+def columns(own_all, head):
+    group = QH // KVH
+    heads = own_all.shape[1] // (2 * (group + 1) * HD)
+    query_at, grad_at = head * group * HD, (heads + head) * group * HD
+    key_at = (2 * heads * group + head) * HD
+    return query_at, grad_at, key_at, key_at + heads * HD
+
+
+def stacked(ref, at, pair):
+    first = at + 2 * pair * HD
+    return jnp.concatenate([ref[:, first : first + HD], ref[:, first + HD : first + 2 * HD]], axis=0)
+
+
+def head_parts(asks, order, own_all, sib_all, far, key_at, value_at):
+    near = order(own_all, sib_all)
+    keys = [ref[:, key_at : key_at + HD] for ref in near]
+    values = [ref[:, value_at : value_at + HD] for ref in near]
+    if asks:
+        distant = order(*far) if len(far) == 2 else far
+        keys = [ref[:, :HD] for ref in distant] + keys
+        values = [ref[:, HD:] for ref in distant] + values
+    return near, jnp.concatenate(keys, axis=0), jnp.concatenate(values, axis=0)
+
+
+def soften(keys, values, q, g, hide, distant, power):
+    scores = contract(keys, q, 1, 1)
+    prob_grad = contract(values, g, 1, 1)
+    hide = jnp.concatenate([hide, hide], axis=1)
+    if distant:
+        scores = jnp.concatenate([scores[:distant], scores[distant:] + hide], axis=0)
+    else:
+        scores = scores + hide
+    peak = jnp.max(scores, axis=0, keepdims=True)
+    exps = jnp.exp2((scores - peak) * power)
+    probs = exps * (1.0 / jnp.sum(exps, axis=0, keepdims=True))
+    delta = jnp.sum(probs * prob_grad, axis=0, keepdims=True)
+    score_grad = (probs * (prob_grad - delta)).astype(jnp.bfloat16)
+    return probs.astype(jnp.bfloat16), score_grad
+
+
+def accumulate(sums, slot, value):
+    sums[slot] = value if sums[slot] is None else sums[slot] + value
+
+
+def attend_kernel(unit, place, bias, own_all, sib_all, *refs):
+    refs = list(refs)
+    far = [refs.pop(0) for _ in range(unit["far"])]
+    split = unit["told"] == 2
+    outs = refs[-5 if not split else -7 :]
+    dq_own, dq_sib, near_own, near_sib, out = outs[:5]
+    head = unit["head"]
+    rows = own_all.shape[0]
+    group = QH // KVH
+    scaling = 1.0 / math.sqrt(HD)
+    power = scaling * LOG2E
+    low = jnp.bfloat16
+    query_at, grad_at, key_at, value_at = columns(own_all, head)
+
+    def body(asks, order):
+        if not asks and unit["later"] is not None:
+            _, _, later_key, later_value = columns(own_all, unit["later"])
+            for half, ref in enumerate(order(own_all, sib_all)):
+                spot = slice(half * rows, (half + 1) * rows)
+                out[spot, :HD] = ref[:, later_key : later_key + HD]
+                out[spot, HD:] = ref[:, later_value : later_value + HD]
+        distant = 2 * rows if asks else 0
+        near, keys, values = head_parts(asks, order, own_all, sib_all, far, key_at, value_at)
+        partial_only = split and asks
+        keys_t = None if partial_only else keys.T
+        dk, dv, told = [None, None], [None, None], [None, None]
+        for pair in range(group // 2):
+            for side in range(2):
+                q = stacked(near[side], query_at, pair)
+                g = stacked(near[side], grad_at, pair)
+                count = distant + (side + 1) * rows
+                hide = bias[: (side + 1) * rows, side * rows : (side + 1) * rows]
+                probs, score_grad = soften(keys[:count], values[:count], q, g, hide, distant, power)
+                if partial_only:
+                    slot = pair * 2 + side
+                    outs[5][slot, :count] = probs
+                    outs[6][slot, :count] = score_grad
+                    wanted = order(0, rows)[0]
+                    accumulate(told, 0, contract(score_grad[wanted : wanted + rows], q, 1, 0))
+                    accumulate(told, 1, contract(probs[wanted : wanted + rows], g, 1, 0))
+                    continue
+                accumulate(dv, side, contract(probs, g, 1, 0))
+                accumulate(dk, side, contract(score_grad, q, 1, 0))
+                dq = (contract(keys_t[:, :count], score_grad, 1, 0) * scaling).T.astype(low)
+                target = order(dq_own, dq_sib)[side]
+                for member in range(2):
+                    at = (pair * 2 + member) * HD
+                    target[:, at : at + HD] = dq[member * rows : (member + 1) * rows]
+        if partial_only:
+            out[:, :HD] = (told[0] * scaling).astype(low)
+            out[:, HD:] = told[1].astype(low)
+            return
+        for slot, (lo, hi) in enumerate((dk, dv)):
+            size = scaling if slot == 0 else 1.0
+            spot = slice(slot * HD, (slot + 1) * HD)
+            first, second = order(near_own, near_sib)
+            first[:, spot] = (lo[distant:] + hi[distant : distant + rows]) * size
+            second[:, spot] = hi[distant + rows :] * size
+            if asks:
+                out[:, spot] = ((lo[:distant] + hi[:distant]) * size).astype(low)
+
+    specialise(place, body)
+
+
+def settle_kernel(unit, place, own_all, sib_all, *refs):
+    refs = list(refs)
+    far = [refs.pop(0) for _ in range(unit["far"])]
+    dq_own_in, dq_sib_in, near_own_in, near_sib_in, probs_in, grads_in = refs[:6]
+    dq_own, back, near_own, out = refs[6:]
+    rows = own_all.shape[0]
+    group = QH // KVH
+    scaling = 1.0 / math.sqrt(HD)
+    low = jnp.bfloat16
+    query_at, grad_at, key_at, value_at = columns(own_all, unit["head"])
+
+    def body(asks, order):
+        if not asks:
+            dq_own[...] = dq_own_in[...]
+            near_own[...] = near_own_in[...]
+            back[:, : group * HD] = dq_sib_in[...]
+            back[:, group * HD :] = near_sib_in[...].astype(low)
+            return
+        near, keys, _ = head_parts(asks, order, own_all, sib_all, far, key_at, value_at)
+        keys_t = keys.T
+        distant = 2 * rows
+        dk, dv, told = [None, None], [None, None], [None, None]
+        for pair in range(group // 2):
+            for side in range(2):
+                slot = pair * 2 + side
+                count = distant + (side + 1) * rows
+                q = stacked(near[side], query_at, pair)
+                g = stacked(near[side], grad_at, pair)
+                probs, score_grad = probs_in[slot, :count], grads_in[slot, :count]
+                wanted = order(0, rows)[1]
+                accumulate(told, 0, contract(score_grad[wanted : wanted + rows], q, 1, 0))
+                accumulate(told, 1, contract(probs[wanted : wanted + rows], g, 1, 0))
+                accumulate(dv, side, contract(probs[distant:], g, 1, 0))
+                accumulate(dk, side, contract(score_grad[distant:], q, 1, 0))
+                dq = (contract(keys_t[:, :count], score_grad, 1, 0) * scaling).T.astype(low)
+                target = order(dq_own, back)[side]
+                for member in range(2):
+                    at = (pair * 2 + member) * HD
+                    target[:, at : at + HD] = dq[member * rows : (member + 1) * rows]
+        for slot, (lo, hi) in enumerate((dk, dv)):
+            size = scaling if slot == 0 else 1.0
+            at = slot * HD
+            targets = order((near_own, at), (back, group * HD + at))
+            for (target, spot), value in zip(targets, (lo + hi[:rows], hi[rows:])):
+                target[:, spot : spot + HD] = (value * size).astype(target.dtype)
+            out[:, at : at + HD] = (told[slot] * size).astype(low)
+
+    specialise(place, body)
+
+
+def fold_kernel(count, place, *refs):
+    nears, tolds, back = refs[:count], refs[count : 2 * count], refs[-1]
+    core = place[0] % 2
+    hears = place[0] // 2 == 0
+    rows, width = nears[0].shape
+    at = pl.multiple_of((1 - core) * rows, rows)
+    for index in range(count):
+        told = jnp.where(hears, tolds[index][pl.ds(at, rows), :].astype(jnp.float32), 0.0)
+        back[:, index * width : (index + 1) * width] = (nears[index][...] + told).astype(back.dtype)
+
+
+def join_kernel(units, place, *refs):
+    outs, (sums, sems) = refs[-5:-2], refs[-2:]
+    core = place[0] % 2
+    hears = place[0] // 2 == 0
+    group = QH // KVH
+    halves = [out.shape[1] // 2 for out in outs]
+    amount = len(units)
+    late = units[0]["told"] == 2
+    copies = []
+
+    def write(source, out, start, width):
+        target = out.at[:, pl.ds(pl.multiple_of(start, HD), width)]
+        copies.append(pltpu.make_async_copy(source, target, sems.at[len(copies)]))
+        copies[-1].start()
+
+    for index, unit in enumerate(units):
+        width = group * HD
+        at = unit["head"] * width
+        sib_part = refs[amount + index]
+        write(refs[index], outs[0], core * halves[0] + at, width)
+        write(sib_part.at[:, :width], outs[0], (1 - core) * halves[0] + at, width)
+    own_rows = pl.multiple_of(core * refs[0].shape[0], HD)
+    for index, unit in enumerate(units):
+        near, told = refs[2 * amount + index], refs[3 * amount + index]
+        rows = near.shape[0]
+        heard = told[...] if late else told[pl.ds(own_rows, rows), :]
+        total = near[...] + jnp.where(hears, heard.astype(jnp.float32), 0.0)
+        sums[index] = total.astype(sums.dtype)
+        for slot in range(2):
+            start = core * halves[1] + unit["head"] * HD
+            write(sums.at[index, :, slot * HD : (slot + 1) * HD], outs[1 + slot], start, HD)
+    other = refs[4 * amount]
+    if late:
+        told = refs[4 * amount + 1]
+        rows = told.shape[0]
+        total = other[:, group * HD :].astype(jnp.float32) + jnp.where(
+            hears, told[...].astype(jnp.float32), 0.0
+        )
+        sums[amount] = total.astype(sums.dtype)
+        other = sums.at[amount]
+    for index, unit in enumerate(units):
+        for slot in range(2):
+            start = (1 - core) * halves[1] + unit["head"] * HD
+            at = (2 * index + slot) * HD
+            write(other.at[:, at : at + HD], outs[1 + slot], start, HD)
+    for copy in copies:
+        copy.wait()
+
+
+def local_call(kernel, outs, args, scratch=(), flops=0, space=pltpu.VMEM, aliases=None, out_space=pltpu.VMEM, in_spaces=None):
+    specs = [pl.BlockSpec(memory_space=pltpu.SMEM)]
+    specs += [pl.BlockSpec(memory_space=kind) for kind in in_spaces or [space] * (len(args) - 1)]
+    return pl.pallas_call(
+        kernel,
+        out_shape=tuple(outs),
+        in_specs=specs,
+        out_specs=tuple(pl.BlockSpec(memory_space=out_space) for _ in outs),
+        scratch_shapes=scratch,
+        input_output_aliases=aliases or {},
+        compiler_params=pltpu.CompilerParams(vmem_limit_bytes=VMEM_BYTES),
+        cost_estimate=pl.CostEstimate(flops=flops, transcendentals=0, bytes_accessed=0),
+    )(*args)
+
+
+def plan_units():
+    count = KVH // 2
+    return [
+        {
+            "head": head,
+            "far": 2 if head < LAG else 1,
+            "told": 2 if head == count - 1 else 1,
+            "later": head + LAG if head + LAG < count else None,
+        }
+        for head in range(count)
+    ]
+
+
+def on_pair(query_rows, key_rows, value_rows, out_grad, question_lengths):
+    rows = query_rows.shape[0]
+    group = QH // KVH
+    low = jnp.bfloat16
+    full = jnp.float32
+    shape = jax.ShapeDtypeStruct
+    units = plan_units()
+    count = len(units)
+    sib = [(0, 1), (1, 0), (2, 3), (3, 2)]
+    same = [(0, 2), (1, 3), (2, 0), (3, 1)]
+    cross = [(0, 3), (1, 2), (2, 1), (3, 0)]
+    link = shape((rows, 2 * HD), low)
+    wide = shape((rows, query_rows.shape[1] + key_rows.shape[1]), low)
+    block = shape((group, 4 * rows, 2 * rows), low)
+
+    def send(value, perm):
+        return lax.ppermute(value, "sp", perm)
+
+    place = lax.axis_index("sp").astype(jnp.int32).reshape(1)
+    whole = (query_rows, out_grad, key_rows, value_rows, question_lengths)
+    fixed = tuple(pltpu.with_memory_space_constraint(value, pltpu.HBM) for value in whole)
+    *packs, sib_send = local_call(
+        pack_kernel, [link] * (2 * LAG) + [wide], (place, *fixed[:4]), space=pltpu.HBM,
+        scratch=[pltpu.SemaphoreType.DMA((4 * LAG + 4,))],
+    )
+    far = []
+    for chunk in range(LAG):
+        far.append((send(packs[2 * chunk], same), send(packs[2 * chunk + 1], cross)))
+    sib_all = send(sib_send, sib)
+    own_all, bias = local_call(
+        stage_kernel, [wide, shape((2 * rows, 2 * rows), full)], (place, *fixed),
+        space=pltpu.HBM,
+        scratch=[
+            pltpu.SMEM(question_lengths.shape, jnp.int32), pltpu.SemaphoreType.DMA((5,)),
+        ],
+    )
+    wings = [shape((rows, group * HD), low)] * 2
+    near = shape((rows, 2 * HD), full)
+    dq_own, dq_sib, near_own, near_sib = [], [], [], []
+    for index, unit in enumerate(units):
+        split = unit["told"] == 2
+        outs = local_call(
+            partial(attend_kernel, unit),
+            [*wings, near, near, link if split else shape((2 * rows, 2 * HD), low)]
+            + ([block, block] if split else []),
+            (place, bias, own_all, sib_all, *far[index]),
+            flops=group * 10 * HD * 2 * rows * 4 * rows,
+        )
+        told = send(outs[4], same)
+        if split:
+            outs = local_call(
+                partial(settle_kernel, unit),
+                [wings[0], shape((rows, (group + 2) * HD), low), near, link],
+                (place, own_all, sib_all, *far[index], *outs[:4], *outs[5:]),
+                flops=group * 4 * HD * 2 * rows * 4 * rows,
+            )
+            told_cross = send(outs[3], cross)
+            back_last = send(outs[1], sib)
+            dq_last, near_last, told_last = outs[0], outs[2], told
+        else:
+            far.append((told,))
+            dq_own.append(outs[0])
+            dq_sib.append(send(outs[1], sib))
+            near_own.append(outs[2])
+            near_sib.append(outs[3])
+    heard = [value[0] for value in far[LAG:]]
+    back_keys, = local_call(
+        partial(fold_kernel, count - 1), [shape((rows, (count - 1) * 2 * HD), low)],
+        (place, *near_sib, *heard),
+    )
+    back_keys = send(back_keys, sib)
+    shapes = [shape(value.shape, low) for value in (query_rows, key_rows, value_rows)]
+
+    def join(part, args, results):
+        spaces = [pltpu.VMEM] * len(args) + [pltpu.HBM] * len(results)
+        return local_call(
+            partial(join_kernel, part), shapes, (place, *args, *results),
+            aliases={1 + len(args) + i: i for i in range(len(results))},
+            in_spaces=spaces, out_space=pltpu.HBM,
+            scratch=[
+                pltpu.VMEM((len(part) + 1, rows, 2 * HD), low),
+                pltpu.SemaphoreType.DMA((6 * len(part),)),
+            ],
+        )
+
+    results = join(units[:-1], (*dq_own, *dq_sib, *near_own, *heard, back_keys), ())
+    results = join(
+        units[-1:], (dq_last, back_last, near_last, told_last, back_last, told_cross),
+        results,
+    )
+    return tuple(results)
+
+
 def solution(mesh):
+    paired = mesh.shape["sp"] == 4
+    rows = P(("grp", "sp"), None)
     return jax.shard_map(
-        on_device,
+        on_pair if paired else on_device,
         mesh=mesh,
-        in_specs=(
-            P(("grp", "sp"), None),
-            P(("grp", "sp"), None),
-            P(("grp", "sp"), None),
-            P(("grp", "sp"), None),
-            P("grp"),
-        ),
-        out_specs=(P(("grp", "sp"), None), P(("grp", "sp"), None), P(("grp", "sp"), None)),
+        in_specs=(rows, rows, rows, rows, P("grp")),
+        out_specs=(rows, rows, rows),
         check_vma=False,
     )

time: 118 us -> 39 us (0.33)
  waiting for transfers between devices: 44 us -> 12.9 us
  local copies, waits for them, and re-layouts: 21.7 us -> 0 us
  matrix products: 21 us -> 0 us
  starting transfers between devices: 25.2 us -> 13.2 us
  Pallas kernels: 0 us -> 11.8 us
  other arithmetic: 4.36 us -> 0 us
    all_to_all x7 -> x0, waiting for transfers between devices: 44 us -> none  [the longest x1 12.3 us: on_device(): lax.all_to_all(query_local, 'sp', split_axis=0, concat_axis=1, tiled=True)]
    all_to_all x7 -> x0, starting transfers between devices: 25.2 us -> none  [the longest x1 4.26 us: on_device(): lax.all_to_all(widen(key_rows, copies), 'sp', split_axis=1, concat_axis=0...]
    dot_general x6 -> x0, matrix products: 21 us -> none  [the longest x1 5.91 us: weighted_values(): jnp.einsum('kgbs,skd->bkgd', probs_b, value_block, preferred_element_type...]
    ppermute x0 -> x15, starting transfers between devices: none -> 13.2 us  [send(): return lax.ppermute(value, 'sp', perm)]
    ppermute x0 -> x15, waiting for transfers between devices: none -> 12.9 us  [send(): return lax.ppermute(value, 'sp', perm)]
    all_to_all x8 -> x0, local copies, waits for them, and re-layouts: 11.9 us -> none  [the longest x1 2.29 us: on_device(): lax.all_to_all(out_grad, 'sp', split_axis=1, concat_axis=0, tiled=True)]
    pallas_call x0 -> x10, Pallas kernels: none -> 11.8 us  [local_call(): pl.pallas_call(kernel, out_shape=tuple(outs), in_specs=specs, out_specs=t...]
    unnamed x13 -> x0, local copies, waits for them, and re-layouts: 4.96 us -> none
  transfers between devices with their start and end apart: 7 -> 15, of which waited for: 5 -> 8; matrix products, arithmetic and copies ran while one was open for 26% -> 0% of each run, Pallas kernels for 0% -> 20%
where the time goes in v1:
time: 39 us; the launch traced here: 38.8 us
  starting transfers between devices  13.2 us (34%)
  waiting for transfers between devices  12.9 us (33%)
  Pallas kernels  11.8 us (30%)
  between operations  0.9 us (2%)
    ppermute x15, starting transfers between devices, send(): return lax.ppermute(value, 'sp', perm)  13.2 us
    ppermute x15, waiting for transfers between devices, send(): return lax.ppermute(value, 'sp', perm)  12.9 us
    pallas_call x10, Pallas kernels, local_call(): pl.pallas_call(kernel, out_shape=tuple(outs), in_specs=specs, out_specs=t...  11.8 us
  transfers between devices with their start and end apart: 15, of which 8 were waited for; matrix products, arithmetic and copies ran while one was open for 0% of the time, Pallas kernels for 20%

profile of v1, /device:TPU:0, one launch (start us, length us, event | category | flops | bytes accessed | tf_op | source)
XLA Modules:
  0.0 38.8 jit_solution(12438636542754505144)
XLA Ops:
  0.6 1.5 %shard_map.77 = (bf16[128,256]{1,0:T(8,128)(2,1)S(1)}, bf16[128,256]{1,0:T(8,128)(2,1)S(1)}, bf16[128,256]{1,0:T(8,128)(2,1)S(1)}, bf16[128,256]{1,0:T(8,128)(2,1)S(1)}, bf16[128,5120]{1,0:T(8,128)(2,1)S(1)}) custom-call(s32[1]{0:T(128)} %bitcast.place, bf16[128,4096]{1,0:T(8,128)(2,1)} %queries.3, bf16[128,4096]{1,0:T(8,128)(2,1)} %grads.3, ...), custom_call_target="tpu_custom_call" | custom-call | tf_op jit(solution)/shard_map/pallas_call | solution.py:463
  2.2 0.6 %collective-permute-start = (bf16[128,5120]{1,0:T(8,128)(2,1)S(1)}, bf16[128,5120]{1,0:T(8,128)(2,1)S(1)}, u32[]{:S(2)}, u32[]{:S(2)}) collective-permute-start(bf16[128,5120]{1,0:T(8,128)(2,1)S(1)} %get-tuple-element.40), channel_id=1, source_target_pairs={{0,1},{1,0},{2,3},{3,2},{4,5},{5,4},{6,7},{7,6},{8,9},{9,8},{10,11... | collective-permute-start | bytes 3932168 | tf_op jit(solution)/shard_map/ppermute | solution.py:504
  2.7 2.6 %collective-permute-start.7 = (bf16[128,256]{1,0:T(8,128)(2,1)S(1)}, bf16[128,256]{1,0:T(8,128)(2,1)S(1)}, u32[]{:S(2)}, u32[]{:S(2)}) collective-permute-start(bf16[128,256]{1,0:T(8,128)(2,1)S(1)} %get-tuple-element.56), channel_id=1, source_target_pairs={{0,2},{1,3},{2,0},{3,1},{4,6},{5,7},{6,4},{7,5},{8,10},{9,11},{10,... | collective-permute-start | bytes 196616 | tf_op jit(solution)/shard_map/ppermute | solution.py:504
  5.4 1.3 %shard_map.76 = (bf16[128,5120]{1,0:T(8,128)(2,1)S(1)}, f32[256,256]{1,0:T(8,128)S(1)}) custom-call(s32[1]{0:T(128)} %bitcast.place, bf16[128,4096]{1,0:T(8,128)(2,1)} %queries.3, bf16[128,4096]{1,0:T(8,128)(2,1)} %grads.3, bf16[128,1024]{1,0:T(8,128)(2,1)} %keys.3, bf16[128,1024]{1,0:T(8,128)(2,1)} %values.3, s32[8]{0:T(128)} %lengths.1), custom_call_target="tpu_custom_call" | custom-call | tf_op jit(solution)/shard_map/pallas_call | solution.py:463
  6.7 1.3 %collective-permute-done.7.refs_0_ = bf16[128,256]{1,0:T(8,128)(2,1)S(1)} collective-permute-done((bf16[128,256]{1,0:T(8,128)(2,1)S(1)}, bf16[128,256]{1,0:T(8,128)(2,1)S(1)}, u32[]{:S(2)}, u32[]{:S(2)}) %collective-permute-start.7) | collective-permute-done | bytes 65568 | tf_op jit(solution)/shard_map/ppermute | solution.py:504
  8.0 1.4 %collective-permute-done.8.refs_1_ = bf16[128,256]{1,0:T(8,128)(2,1)S(1)} collective-permute-done((bf16[128,256]{1,0:T(8,128)(2,1)S(1)}, bf16[128,256]{1,0:T(8,128)(2,1)S(1)}, u32[]{:S(2)}, u32[]{:S(2)}) %collective-permute-start.8) | collective-permute-done | bytes 65568 | tf_op jit(solution)/shard_map/ppermute | solution.py:504
  9.4 1.7 %shard_map.81 = (bf16[128,512]{1,0:T(8,128)(2,1)S(1)}, bf16[128,512]{1,0:T(8,128)(2,1)S(1)}, f32[128,256]{1,0:T(8,128)S(1)}, f32[128,256]{1,0:T(8,128)S(1)}, bf16[256,256]{1,0:T(8,128)(2,1)S(1)}) custom-call(s32[1]{0:T(128)} %bitcast.place, f32[256,256]{1,0:T(8,128)S(1)} %get-tuple-element.41.bias, bf16[128,5120]{1,0:T(8,128)(2,1)S(1)} %get-tuple-element.39.own_all, ...), custom_call_target="tpu_custom_call" | custom-call | flops 671088640 | tf_op jit(solution)/shard_map/pallas_call | solution.py:463
  11.1 2.1 %collective-permute-start.9 = (bf16[256,256]{1,0:T(8,128)(2,1)S(1)}, bf16[256,256]{1,0:T(8,128)(2,1)S(1)}, u32[]{:S(2)}, u32[]{:S(2)}) collective-permute-start(bf16[256,256]{1,0:T(8,128)(2,1)S(1)} %get-tuple-element.60), channel_id=1, source_target_pairs={{0,2},{1,3},{2,0},{3,1},{4,6},{5,7},{6,4},{7,5},{8,10},{9,11},{10,... | collective-permute-start | bytes 393224 | tf_op jit(solution)/shard_map/ppermute | solution.py:504
  13.2 1.3 %collective-permute-start.2 = (bf16[128,256]{1,0:T(8,128)(2,1)S(1)}, bf16[128,256]{1,0:T(8,128)(2,1)S(1)}, u32[]{:S(2)}, u32[]{:S(2)}) collective-permute-start(bf16[128,256]{1,0:T(8,128)(2,1)S(1)} %get-tuple-element.43), channel_id=1, source_target_pairs={{0,3},{1,2},{2,1},{3,0},{4,7},{5,6},{6,5},{7,4},{8,11},{9,10},{10,... | collective-permute-start | bytes 196616 | tf_op jit(solution)/shard_map/ppermute | solution.py:504
  14.6 4.3 %collective-permute-done.1.refs_0_ = bf16[128,256]{1,0:T(8,128)(2,1)S(1)} collective-permute-done((bf16[128,256]{1,0:T(8,128)(2,1)S(1)}, bf16[128,256]{1,0:T(8,128)(2,1)S(1)}, u32[]{:S(2)}, u32[]{:S(2)}) %collective-permute-start.1) | collective-permute-done | bytes 65568 | tf_op jit(solution)/shard_map/ppermute | solution.py:504
  18.9 0.7 %collective-permute-done.2.refs_1_ = bf16[128,256]{1,0:T(8,128)(2,1)S(1)} collective-permute-done((bf16[128,256]{1,0:T(8,128)(2,1)S(1)}, bf16[128,256]{1,0:T(8,128)(2,1)S(1)}, u32[]{:S(2)}, u32[]{:S(2)}) %collective-permute-start.2) | collective-permute-done | bytes 65568 | tf_op jit(solution)/shard_map/ppermute | solution.py:504
  19.6 1.9 %shard_map.78 = (bf16[128,512]{1,0:T(8,128)(2,1)S(1)}, bf16[128,512]{1,0:T(8,128)(2,1)S(1)}, f32[128,256]{1,0:T(8,128)S(1)}, f32[128,256]{1,0:T(8,128)S(1)}, bf16[256,256]{1,0:T(8,128)(2,1)S(1)}) custom-call(s32[1]{0:T(128)} %bitcast.place, f32[256,256]{1,0:T(8,128)S(1)} %get-tuple-element.41.bias, bf16[128,5120]{1,0:T(8,128)(2,1)S(1)} %get-tuple-element.39.own_all, ...), custom_call_target="tpu_custom_call" | custom-call | flops 671088640 | tf_op jit(solution)/shard_map/pallas_call | solution.py:463
  21.5 2.3 %collective-permute-start.3 = (bf16[256,256]{1,0:T(8,128)(2,1)S(1)}, bf16[256,256]{1,0:T(8,128)(2,1)S(1)}, u32[]{:S(2)}, u32[]{:S(2)}) collective-permute-start(bf16[256,256]{1,0:T(8,128)(2,1)S(1)} %get-tuple-element.44), channel_id=1, source_target_pairs={{0,2},{1,3},{2,0},{3,1},{4,6},{5,7},{6,4},{7,5},{8,10},{9,11},{10,... | collective-permute-start | bytes 393224 | tf_op jit(solution)/shard_map/ppermute | solution.py:504
  23.8 1.7 %shard_map.82 = (bf16[128,512]{1,0:T(8,128)(2,1)S(1)}, bf16[128,512]{1,0:T(8,128)(2,1)S(1)}, f32[128,256]{1,0:T(8,128)S(1)}, f32[128,256]{1,0:T(8,128)S(1)}, bf16[256,256]{1,0:T(8,128)(2,1)S(1)}) custom-call(s32[1]{0:T(128)} %bitcast.place, f32[256,256]{1,0:T(8,128)S(1)} %get-tuple-element.41.bias, bf16[128,5120]{1,0:T(8,128)(2,1)S(1)} %get-tuple-element.39.own_all, ...), custom_call_target="tpu_custom_call" | custom-call | flops 671088640 | tf_op jit(solution)/shard_map/pallas_call | solution.py:463
  25.5 0.9 %collective-permute-start.13 = (bf16[256,256]{1,0:T(8,128)(2,1)S(1)}, bf16[256,256]{1,0:T(8,128)(2,1)S(1)}, u32[]{:S(2)}, u32[]{:S(2)}) collective-permute-start(bf16[256,256]{1,0:T(8,128)(2,1)S(1)} %get-tuple-element.68), channel_id=1, source_target_pairs={{0,2},{1,3},{2,0},{3,1},{4,6},{5,7},{6,4},{7,5},{8,10},{9,11},{10,... | collective-permute-start | bytes 393224 | tf_op jit(solution)/shard_map/ppermute | solution.py:504
  26.9 0.8 %collective-permute-done.3.refs_0_.refs_4_.refs_10_ = bf16[256,256]{1,0:T(8,128)(2,1)S(1)} collective-permute-done((bf16[256,256]{1,0:T(8,128)(2,1)S(1)}, bf16[256,256]{1,0:T(8,128)(2,1)S(1)}, u32[]{:S(2)}, u32[]{:S(2)}) %collective-permute-start.3) | collective-permute-done | bytes 131104 | tf_op jit(solution)/shard_map/ppermute | solution.py:504
  27.7 1.7 %shard_map.79 = (bf16[128,512]{1,0:T(8,128)(2,1)S(1)}, bf16[128,512]{1,0:T(8,128)(2,1)S(1)}, f32[128,256]{1,0:T(8,128)S(1)}, f32[128,256]{1,0:T(8,128)S(1)}, bf1...) custom-call(s32[1]{0:T(128)} %bitcast.place, ...), custom_call_target="tpu_custom_call" | custom-call | flops 671088640 | tf_op jit(solution)/shard_map/pallas_call | solution.py:463
  29.4 1.5 %collective-permute-done.13.refs_5_.refs_11_ = bf16[256,256]{1,0:T(8,128)(2,1)S(1)} collective-permute-done((bf16[256,256]{1,0:T(8,128)(2,1)S(1)}, bf16[256,256]{1,0:T(8,128)(2,1)S(1)}, u32[]{:S(2)}, u32[]{:S(2)}) %collective-permute-start.13) | collective-permute-done | bytes 131104 | tf_op jit(solution)/shard_map/ppermute | solution.py:504
  31.1 0.5 %collective-permute-start.4 = (bf16[128,768]{1,0:T(8,128)(2,1)S(1)}, bf16[128,768]{1,0:T(8,128)(2,1)S(1)}, u32[]{:S(2)}, u32[]{:S(2)}) collective-permute-start(bf16[128,768]{1,0:T(8,128)(2,1)S(1)} %get-tuple-element.52), channel_id=1, source_target_pairs={{0,1},{1,0},{2,3},{3,2},{4,5},{5,4},{6,7},{7,6},{8,9},{9,8},{10,11... | collective-permute-start | bytes 589832 | tf_op jit(solution)/shard_map/ppermute | solution.py:504
  31.8 2.0 %collective-permute-start.5 = (bf16[128,256]{1,0:T(8,128)(2,1)S(1)}, bf16[128,256]{1,0:T(8,128)(2,1)S(1)}, u32[]{:S(2)}, u32[]{:S(2)}) collective-permute-start(bf16[128,256]{1,0:T(8,128)(2,1)S(1)} %get-tuple-element.54), channel_id=1, source_target_pairs={{0,2},{1,3},{2,0},{3,1},{4,6},{5,7},{6,4},{7,5},{8,10},{9,11},{10,... | collective-permute-start | bytes 196616 | tf_op jit(solution)/shard_map/ppermute | solution.py:504
  33.9 1.2 %shard_map.84 = (bf16[128,4096]{1,0:T(8,128)(2,1)}, bf16[128,1024]{1,0:T(8,128)(2,1)}, bf16[128,1024]{1,0:T(8,128)(2,1)}) custom-call(s32[1]{0:T(128)} %bitcast.place, bf16[128,512]{1,0:T(8,128)(2,1)S(1)} %get-tuple-element.58.refs_0_, bf16[128,512]{1,0:T(8,128)(2,1)S(1)} %get-tuple-element.59.refs_1_, bf16[128,512]{1,0:T(8,128)(2,1)S(1)} %get-tuple-element.61.refs_2_, ...), custom_call_target="tpu_custom_call" | custom-call | tf_op jit(solution)/shard_map/pallas_call | solution.py:463
  35.1 1.4 %collective-permute-done.5.refs_3_ = bf16[128,256]{1,0:T(8,128)(2,1)S(1)} collective-permute-done((bf16[128,256]{1,0:T(8,128)(2,1)S(1)}, bf16[128,256]{1,0:T(8,128)(2,1)S(1)}, u32[]{:S(2)}, u32[]{:S(2)}) %collective-permute-start.5) | collective-permute-done | bytes 65568 | tf_op jit(solution)/shard_map/ppermute | solution.py:504
  36.5 1.4 %collective-permute-done.6.refs_5_ = bf16[128,256]{1,0:T(8,128)(2,1)S(1)} collective-permute-done((bf16[128,256]{1,0:T(8,128)(2,1)S(1)}, bf16[128,256]{1,0:T(8,128)(2,1)S(1)}, u32[]{:S(2)}, u32[]{:S(2)}) %collective-permute-start.6) | collective-permute-done | bytes 65568 | tf_op jit(solution)/shard_map/ppermute | solution.py:504
  37.8 0.8 %shard_map.85 = (bf16[128,4096]{1,0:T(8,128)(2,1)}, bf16[128,1024]{1,0:T(8,128)(2,1)}, bf16[128,1024]{1,0:T(8,128)(2,1)}) custom-call(s32[1]{0:T(128)} %bitcast.place, bf16[128,512]{1,0:T(8,128)(2,1)S(1)} %get-tuple-element.51.refs_0_, ...), custom_call_target="tpu_custom_call", output_to_operand_aliasing={{0}: (7, {}), {1}: (8, {}), {2}: (9, {})} | custom-call | tf_op jit(solution)/shard_map/pallas_call | solution.py:463
  (16 shorter events, 1.0 us)
Async XLA Ops:
  2.2 7.2 %collective-permute-start = (bf16[128,5120]{1,0:T(8,128)(2,1)S(1)}, bf16[128,5120]{1,0:T(8,128)(2,1)S(1)}, u32[]{:S(2)}, u32[]{:S(2)}) collective-permute-start(bf16[128,5120]{1,0:T(8,128)(2,1)S(1)} %get-tuple-element.40), channel_id=1, source_target_pairs={{0,1},{1,0},{2,3},{3,2},{4,5},{5,4},{6,7},{7,6},{8,9},{9,8},{10,11... | collective-permute-start | bytes 3932168 | tf_op jit(solution)/shard_map/ppermute | solution.py:504
  2.7 5.3 %collective-permute-start.7 = (bf16[128,256]{1,0:T(8,128)(2,1)S(1)}, bf16[128,256]{1,0:T(8,128)(2,1)S(1)}, u32[]{:S(2)}, u32[]{:S(2)}) collective-permute-start(bf16[128,256]{1,0:T(8,128)(2,1)S(1)} %get-tuple-element.56), channel_id=1, source_target_pairs={{0,2},{1,3},{2,0},{3,1},{4,6},{5,7},{6,4},{7,5},{8,10},{9,11},{10,... | collective-permute-start | bytes 196616 | tf_op jit(solution)/shard_map/ppermute | solution.py:504
  5.3 4.1 %collective-permute-start.8 = (bf16[128,256]{1,0:T(8,128)(2,1)S(1)}, bf16[128,256]{1,0:T(8,128)(2,1)S(1)}, u32[]{:S(2)}, u32[]{:S(2)}) collective-permute-start(bf16[128,256]{1,0:T(8,128)(2,1)S(1)} %get-tuple-element.57), channel_id=1, source_target_pairs={{0,3},{1,2},{2,1},{3,0},{4,7},{5,6},{6,5},{7,4},{8,11},{9,10},{10,... | collective-permute-start | bytes 196616 | tf_op jit(solution)/shard_map/ppermute | solution.py:504
  11.1 12.8 %collective-permute-start.9 = (bf16[256,256]{1,0:T(8,128)(2,1)S(1)}, bf16[256,256]{1,0:T(8,128)(2,1)S(1)}, u32[]{:S(2)}, u32[]{:S(2)}) collective-permute-start(bf16[256,256]{1,0:T(8,128)(2,1)S(1)} %get-tuple-element.60), channel_id=1, source_target_pairs={{0,2},{1,3},{2,0},{3,1},{4,6},{5,7},{6,4},{7,5},{8,10},{9,11},{10,... | collective-permute-start | bytes 393224 | tf_op jit(solution)/shard_map/ppermute | solution.py:504
  13.2 5.8 %collective-permute-start.1 = (bf16[128,256]{1,0:T(8,128)(2,1)S(1)}, bf16[128,256]{1,0:T(8,128)(2,1)S(1)}, u32[]{:S(2)}, u32[]{:S(2)}) collective-permute-start(bf16[128,256]{1,0:T(8,128)(2,1)S(1)} %get-tuple-element.42), channel_id=1, source_target_pairs={{0,2},{1,3},{2,0},{3,1},{4,6},{5,7},{6,4},{7,5},{8,10},{9,11},{10,... | collective-permute-start | bytes 196616 | tf_op jit(solution)/shard_map/ppermute | solution.py:504
  13.2 6.4 %collective-permute-start.2 = (bf16[128,256]{1,0:T(8,128)(2,1)S(1)}, bf16[128,256]{1,0:T(8,128)(2,1)S(1)}, u32[]{:S(2)}, u32[]{:S(2)}) collective-permute-start(bf16[128,256]{1,0:T(8,128)(2,1)S(1)} %get-tuple-element.43), channel_id=1, source_target_pairs={{0,3},{1,2},{2,1},{3,0},{4,7},{5,6},{6,5},{7,4},{8,11},{9,10},{10,... | collective-permute-start | bytes 196616 | tf_op jit(solution)/shard_map/ppermute | solution.py:504
  21.5 6.2 %collective-permute-start.3 = (bf16[256,256]{1,0:T(8,128)(2,1)S(1)}, bf16[256,256]{1,0:T(8,128)(2,1)S(1)}, u32[]{:S(2)}, u32[]{:S(2)}) collective-permute-start(bf16[256,256]{1,0:T(8,128)(2,1)S(1)} %get-tuple-element.44), channel_id=1, source_target_pairs={{0,2},{1,3},{2,0},{3,1},{4,6},{5,7},{6,4},{7,5},{8,10},{9,11},{10,... | collective-permute-start | bytes 393224 | tf_op jit(solution)/shard_map/ppermute | solution.py:504
  25.5 5.4 %collective-permute-start.13 = (bf16[256,256]{1,0:T(8,128)(2,1)S(1)}, bf16[256,256]{1,0:T(8,128)(2,1)S(1)}, u32[]{:S(2)}, u32[]{:S(2)}) collective-permute-start(bf16[256,256]{1,0:T(8,128)(2,1)S(1)} %get-tuple-element.68), channel_id=1, source_target_pairs={{0,2},{1,3},{2,0},{3,1},{4,6},{5,7},{6,4},{7,5},{8,10},{9,11},{10,... | collective-permute-start | bytes 393224 | tf_op jit(solution)/shard_map/ppermute | solution.py:504
  26.4 5.4 %collective-permute-start.10 = (bf16[128,512]{1,0:T(8,128)(2,1)S(1)}, bf16[128,512]{1,0:T(8,128)(2,1)S(1)}, u32[]{:S(2)}, u32[]{:S(2)}) collective-permute-start(bf16[128,512]{1,0:T(8,128)(2,1)S(1)} %get-tuple-element.62), channel_id=1, source_target_pairs={{0,1},{1,0},{2,3},{3,2},{4,5},{5,4},{6,7},{7,6},{8,9},{9,8},{10,11... | collective-permute-start | bytes 393224 | tf_op jit(solution)/shard_map/ppermute | solution.py:504
  26.4 7.4 %collective-permute-start.11 = (bf16[128,512]{1,0:T(8,128)(2,1)S(1)}, bf16[128,512]{1,0:T(8,128)(2,1)S(1)}, u32[]{:S(2)}, u32[]{:S(2)}) collective-permute-start(bf16[128,512]{1,0:T(8,128)(2,1)S(1)} %get-tuple-element.63), channel_id=1, source_target_pairs={{0,1},{1,0},{2,3},{3,2},{4,5},{5,4},{6,7},{7,6},{8,9},{9,8},{10,11... | collective-permute-start | bytes 393224 | tf_op jit(solution)/shard_map/ppermute | solution.py:504
  31.0 2.9 %collective-permute-start.14 = (bf16[128,768]{1,0:T(8,128)(2,1)S(1)}, bf16[128,768]{1,0:T(8,128)(2,1)S(1)}, u32[]{:S(2)}, u32[]{:S(2)}) collective-permute-start(bf16[128,768]{1,0:T(8,128)(2,1)S(1)} %shard_map.83), channel_id=1, source_target_pairs={{0,1},{1,0},{2,3},{3,2},{4,5},{5,4},{6,7},{7,6},{8,9},{9,8},{10,11... | collective-permute-start | bytes 589832 | tf_op jit(solution)/shard_map/ppermute | solution.py:504
  31.1 6.7 %collective-permute-start.4 = (bf16[128,768]{1,0:T(8,128)(2,1)S(1)}, bf16[128,768]{1,0:T(8,128)(2,1)S(1)}, u32[]{:S(2)}, u32[]{:S(2)}) collective-permute-start(bf16[128,768]{1,0:T(8,128)(2,1)S(1)} %get-tuple-element.52), channel_id=1, source_target_pairs={{0,1},{1,0},{2,3},{3,2},{4,5},{5,4},{6,7},{7,6},{8,9},{9,8},{10,11... | collective-permute-start | bytes 589832 | tf_op jit(solution)/shard_map/ppermute | solution.py:504
  31.7 2.2 %collective-permute-start.12 = (bf16[128,512]{1,0:T(8,128)(2,1)S(1)}, bf16[128,512]{1,0:T(8,128)(2,1)S(1)}, u32[]{:S(2)}, u32[]{:S(2)}) collective-permute-start(bf16[128,512]{1,0:T(8,128)(2,1)S(1)} %get-tuple-element.64), channel_id=1, source_target_pairs={{0,1},{1,0},{2,3},{3,2},{4,5},{5,4},{6,7},{7,6},{8,9},{9,8},{10,11... | collective-permute-start | bytes 393224 | tf_op jit(solution)/shard_map/ppermute | solution.py:504
  31.8 4.7 %collective-permute-start.5 = (bf16[128,256]{1,0:T(8,128)(2,1)S(1)}, bf16[128,256]{1,0:T(8,128)(2,1)S(1)}, u32[]{:S(2)}, u32[]{:S(2)}) collective-permute-start(bf16[128,256]{1,0:T(8,128)(2,1)S(1)} %get-tuple-element.54), channel_id=1, source_target_pairs={{0,2},{1,3},{2,0},{3,1},{4,6},{5,7},{6,4},{7,5},{8,10},{9,11},{10,... | collective-permute-start | bytes 196616 | tf_op jit(solution)/shard_map/ppermute | solution.py:504
  33.8 4.1 %collective-permute-start.6 = (bf16[128,256]{1,0:T(8,128)(2,1)S(1)}, bf16[128,256]{1,0:T(8,128)(2,1)S(1)}, u32[]{:S(2)}, u32[]{:S(2)}) collective-permute-start(bf16[128,256]{1,0:T(8,128)(2,1)S(1)} %get-tuple-element.55), channel_id=1, source_target_pairs={{0,3},{1,2},{2,1},{3,0},{4,7},{5,6},{6,5},{7,4},{8,11},{9,10},{10,... | collective-permute-start | bytes 196616 | tf_op jit(solution)/shard_map/ppermute | solution.py:504

commit v2 on v1

--- a/solution.py
+++ b/solution.py
@@ -13,7 +13,10 @@
 QH = 32
 KVH = 8
 
-LAG = 2
+LAG = 3
+FOLDS = (2, 1)
+STAGGER = [(stage, slot) for stage in range(3) for slot in range(4)]
+STRIP = 64
 VMEM_BYTES = 32 * 1024 * 1024
 
 
@@ -194,40 +197,65 @@
     return pairs
 
 
+def lend_pairs(core, sources, sib_send, own_first):
+    pairs = halves_into(sources, 1 - core, sib_send)
+    group = QH // KVH
+    at = 0
+    for source, width in zip(sources, (group * HD, group * HD, HD, HD)):
+        start = pl.multiple_of(core * (source.shape[1] // 2), HD)
+        pairs.append((source.at[:, pl.ds(start, width)], own_first.at[:, at : at + width]))
+        at += width
+    return pairs
+
+
+def fill_bias(bias, spans, asking):
+    spots = lax.broadcasted_iota(jnp.int32, bias.shape, 1)
+    key_spots = lax.broadcasted_iota(jnp.int32, bias.shape, 0)
+    visible = key_spots <= spots
+    if asking:
+        spot_row = lax.broadcasted_iota(jnp.int32, (1, bias.shape[1]), 1)
+        begin = jnp.zeros((1, bias.shape[1]), jnp.int32)
+        end = jnp.int32(0)
+        for question in range(spans.shape[0]):
+            end = end + spans[question]
+            begin = begin + jnp.where(spot_row >= end, spans[question], 0)
+        visible = visible & (key_spots >= begin)
+    bias[...] = jnp.where(visible, 0.0, HIDDEN)
+
+
 def pack_kernel(place, queries, grads, keys, values, *refs):
-    *sends, sib_send, sems = refs
+    *sends, sib_send, own_first, bias, sems = refs
     core = place[0] % 2
     half = keys.shape[1] // 2
-    pairs = []
-    for index, out in enumerate(sends):
-        chunk, side = index // 2, index % 2
-        base = (core if side == 0 else 1 - core) * half
-        start = pl.multiple_of(base + chunk * HD, HD)
-        pairs.append((keys.at[:, pl.ds(start, HD)], out.at[:, :HD]))
-        pairs.append((values.at[:, pl.ds(start, HD)], out.at[:, HD:]))
-    pairs += halves_into((queries, grads, keys, values), 1 - core, sib_send)
-    for copy in start_all(pairs, sems):
-        copy.wait()
-
-
-def stage_kernel(place, queries, grads, keys, values, lengths, own_all, bias, spans, sems):
-    core = place[0] % 2
-    asking = place[0] // 2
-    pairs = [(lengths, spans)] + halves_into((queries, grads, keys, values), core, own_all)
-    copies = start_all(pairs, sems)
-    copies[0].wait()
-    spots = lax.broadcasted_iota(jnp.int32, bias.shape, 1)
-    key_spots = lax.broadcasted_iota(jnp.int32, bias.shape, 0)
-    spot_row = lax.broadcasted_iota(jnp.int32, (1, bias.shape[1]), 1)
-    begin = jnp.zeros((1, bias.shape[1]), jnp.int32)
-    end = jnp.int32(0)
-    for question in range(lengths.shape[0]):
-        end = end + spans[question]
-        begin = begin + jnp.where(spot_row >= end, spans[question], 0)
-    begin = begin * asking
-    bias[...] = jnp.where((key_spots <= spots) & (key_spots >= begin), 0.0, HIDDEN)
-    for copy in copies[1:]:
-        copy.wait()
+
+    @pl.when(place[0] // 2 == 0)
+    def _():
+        pairs = []
+        for index, out in enumerate(sends):
+            chunk, side = index // 2, index % 2
+            base = (core if side == 0 else 1 - core) * half
+            start = pl.multiple_of(base + chunk * HD, HD)
+            pairs.append((keys.at[:, pl.ds(start, HD)], out.at[:, :HD]))
+            pairs.append((values.at[:, pl.ds(start, HD)], out.at[:, HD:]))
+        pairs += lend_pairs(core, (queries, grads, keys, values), sib_send, own_first)
+        copies = start_all(pairs, sems)
+        fill_bias(bias, None, False)
+        for copy in copies:
+            copy.wait()
+
+
+def lend_kernel(place, queries, grads, keys, values, lengths, *refs):
+    sib_send, own_first, bias, spans, sems = refs[-5:]
+
+    @pl.when(place[0] // 2 == 1)
+    def _():
+        sources = (queries, grads, keys, values)
+        pairs = [(lengths, spans)] + lend_pairs(place[0] % 2, sources, sib_send, own_first)
+        copies = start_all(pairs, sems)
+        copies[0].wait()
+        fill_bias(bias, spans, True)
+        for copy in copies[1:]:
+            copy.wait()
 
 
 def specialise(place, body):
@@ -247,36 +275,65 @@
     return query_at, grad_at, key_at, key_at + heads * HD
 
 
+def head_columns(ref, head):
+    group = QH // KVH
+    if ref.shape[1] == KVH * (group + 1) * HD:
+        return columns(ref, head)
+    return 0, group * HD, 2 * group * HD, (2 * group + 1) * HD
+
+
 def stacked(ref, at, pair):
     first = at + 2 * pair * HD
     return jnp.concatenate([ref[:, first : first + HD], ref[:, first + HD : first + 2 * HD]], axis=0)
 
 
-def head_parts(asks, order, own_all, sib_all, far, key_at, value_at):
-    near = order(own_all, sib_all)
-    keys = [ref[:, key_at : key_at + HD] for ref in near]
-    values = [ref[:, value_at : value_at + HD] for ref in near]
+def head_parts(asks, order, own, sib_all, far, head):
+    near = order((own, *head_columns(own, head)), (sib_all, *head_columns(sib_all, head)))
+    keys = [ref[:, at : at + HD] for ref, _, _, at, _ in near]
+    values = [ref[:, at : at + HD] for ref, _, _, _, at in near]
     if asks:
         distant = order(*far) if len(far) == 2 else far
         keys = [ref[:, :HD] for ref in distant] + keys
         values = [ref[:, HD:] for ref in distant] + values
-    return near, jnp.concatenate(keys, axis=0), jnp.concatenate(values, axis=0)
-
-
-def soften(keys, values, q, g, hide, distant, power):
+    queries = lambda side, pair: stacked(near[side][0], near[side][1], pair)
+    grads = lambda side, pair: stacked(near[side][0], near[side][2], pair)
+    return queries, grads, jnp.concatenate(keys, axis=0), jnp.concatenate(values, axis=0)
+
+
+def fold_rows(op, value):
+    return op(value.reshape(value.shape[0] // 8, 8, value.shape[1]), axis=0)
+
+
+def score(keys, values, q, g, hide, distant):
     scores = contract(keys, q, 1, 1)
-    prob_grad = contract(values, g, 1, 1)
     hide = jnp.concatenate([hide, hide], axis=1)
-    if distant:
-        scores = jnp.concatenate([scores[:distant], scores[distant:] + hide], axis=0)
-    else:
-        scores = scores + hide
-    peak = jnp.max(scores, axis=0, keepdims=True)
-    exps = jnp.exp2((scores - peak) * power)
-    probs = exps * (1.0 / jnp.sum(exps, axis=0, keepdims=True))
-    delta = jnp.sum(probs * prob_grad, axis=0, keepdims=True)
-    score_grad = (probs * (prob_grad - delta)).astype(jnp.bfloat16)
-    return probs.astype(jnp.bfloat16), score_grad
+    parts, peak = [], None
+    for start in range(0, scores.shape[0], STRIP):
+        part = scores[start : start + STRIP]
+        if start >= distant:
+            part = part + hide[start - distant : start - distant + STRIP]
+        parts.append(part)
+        top = fold_rows(jnp.max, part)
+        peak = top if peak is None else jnp.maximum(peak, top)
+    return parts, jnp.max(peak, axis=0, keepdims=True), contract(values, g, 1, 1)
+
+
+def soften(parts, peak, prob_grad, power):
+    exps, total, weighted = [], 0.0, 0.0
+    grads = [prob_grad[i * STRIP : (i + 1) * STRIP] for i in range(len(parts))]
+    for part, grad in zip(parts, grads):
+        exp = jnp.exp2((part - peak) * power)
+        exps.append(exp)
+        total = total + fold_rows(jnp.sum, exp)
+        weighted = weighted + fold_rows(jnp.sum, exp * grad)
+    inverse = 1.0 / jnp.sum(total, axis=0, keepdims=True)
+    delta = jnp.sum(weighted, axis=0, keepdims=True) * inverse
+    probs, score_grads = [], []
+    for exp, grad in zip(exps, grads):
+        prob = exp * inverse
+        probs.append(prob.astype(jnp.bfloat16))
+        score_grads.append((prob * (grad - delta)).astype(jnp.bfloat16))
+    return jnp.concatenate(probs, axis=0), jnp.concatenate(score_grads, axis=0)
 
 
 def accumulate(sums, slot, value):
@@ -287,50 +344,70 @@
     refs = list(refs)
     far = [refs.pop(0) for _ in range(unit["far"])]
     split = unit["told"] == 2
+    copies, own_rest = [], own_all
+    if unit["head"] == 0:
+        *refs, own_rest, sems = refs
+        copies = start_all(halves_into(refs[:4], place[0] % 2, own_rest), sems)
     outs = refs[-5 if not split else -7 :]
     dq_own, dq_sib, near_own, near_sib, out = outs[:5]
     head = unit["head"]
     rows = own_all.shape[0]
-    group = QH // KVH
     scaling = 1.0 / math.sqrt(HD)
     power = scaling * LOG2E
     low = jnp.bfloat16
-    query_at, grad_at, key_at, value_at = columns(own_all, head)
+
+    def pass_on(asks, order):
+        if asks or unit["later"] is None:
+            return
+        _, _, later_key, later_value = columns(sib_all, unit["later"])
+        for half, ref in enumerate(order(own_rest, sib_all)):
+            spot = slice(half * rows, (half + 1) * rows)
+            out[spot, :HD] = ref[:, later_key : later_key + HD]
+            out[spot, HD:] = ref[:, later_value : later_value + HD]
 
     def body(asks, order):
-        if not asks and unit["later"] is not None:
-            _, _, later_key, later_value = columns(own_all, unit["later"])
-            for half, ref in enumerate(order(own_all, sib_all)):
-                spot = slice(half * rows, (half + 1) * rows)
-                out[spot, :HD] = ref[:, later_key : later_key + HD]
-                out[spot, HD:] = ref[:, later_value : later_value + HD]
+        if not copies:
+            pass_on(asks, order)
         distant = 2 * rows if asks else 0
-        near, keys, values = head_parts(asks, order, own_all, sib_all, far, key_at, value_at)
+        queries, grads, keys, values = head_parts(asks, order, own_all, sib_all, far, head)
         partial_only = split and asks
         keys_t = None if partial_only else keys.T
         dk, dv, told = [None, None], [None, None], [None, None]
-        for pair in range(group // 2):
-            for side in range(2):
-                q = stacked(near[side], query_at, pair)
-                g = stacked(near[side], grad_at, pair)
-                count = distant + (side + 1) * rows
-                hide = bias[: (side + 1) * rows, side * rows : (side + 1) * rows]
-                probs, score_grad = soften(keys[:count], values[:count], q, g, hide, distant, power)
-                if partial_only:
-                    slot = pair * 2 + side
-                    outs[5][slot, :count] = probs
-                    outs[6][slot, :count] = score_grad
-                    wanted = order(0, rows)[0]
-                    accumulate(told, 0, contract(score_grad[wanted : wanted + rows], q, 1, 0))
-                    accumulate(told, 1, contract(probs[wanted : wanted + rows], g, 1, 0))
-                    continue
-                accumulate(dv, side, contract(probs, g, 1, 0))
-                accumulate(dk, side, contract(score_grad, q, 1, 0))
-                dq = (contract(keys_t[:, :count], score_grad, 1, 0) * scaling).T.astype(low)
-                target = order(dq_own, dq_sib)[side]
-                for member in range(2):
-                    at = (pair * 2 + member) * HD
-                    target[:, at : at + HD] = dq[member * rows : (member + 1) * rows]
+        held = {}
+
+        def first_stage(slot):
+            pair, side = slot // 2, slot % 2
+            q, g = queries(side, pair), grads(side, pair)
+            count = distant + (side + 1) * rows
+            hide = bias[: (side + 1) * rows, side * rows : (side + 1) * rows]
+            held[slot] = (q, g, *score(keys[:count], values[:count], q, g, hide, distant))
+
+        def second_stage(slot):
+            q, g, scores, peak, prob_grad = held[slot]
+            held[slot] = (q, g, *soften(scores, peak, prob_grad, power))
+
+        def third_stage(slot):
+            pair, side = slot // 2, slot % 2
+            count = distant + (side + 1) * rows
+            q, g, probs, score_grad = held.pop(slot)
+            if partial_only:
+                outs[5][slot, :count] = probs
+                outs[6][slot, :count] = score_grad
+                wanted = order(0, rows)[0]
+                accumulate(told, 0, contract(score_grad[wanted : wanted + rows], q, 1, 0))
+                accumulate(told, 1, contract(probs[wanted : wanted + rows], g, 1, 0))
+                return
+            accumulate(dv, side, contract(probs, g, 1, 0))
+            accumulate(dk, side, contract(score_grad, q, 1, 0))
+            dq = (contract(keys_t[:, :count], score_grad, 1, 0) * scaling).T.astype(low)
+            target = order(dq_own, dq_sib)[side]
+            for member in range(2):
+                at = (pair * 2 + member) * HD
+                target[:, at : at + HD] = dq[member * rows : (member + 1) * rows]
+
+        stages = (first_stage, second_stage, third_stage)
+        for stage, slot in STAGGER:
+            stages[stage](slot)
         if partial_only:
             out[:, :HD] = (told[0] * scaling).astype(low)
             out[:, HD:] = told[1].astype(low)
@@ -345,6 +422,10 @@
                 out[:, spot] = ((lo[:distant] + hi[:distant]) * size).astype(low)
 
     specialise(place, body)
+    if copies:
+        for copy in copies:
+            copy.wait()
+        specialise(place, pass_on)
 
 
 def settle_kernel(unit, place, own_all, sib_all, *refs):
@@ -356,7 +437,6 @@
     group = QH // KVH
     scaling = 1.0 / math.sqrt(HD)
     low = jnp.bfloat16
-    query_at, grad_at, key_at, value_at = columns(own_all, unit["head"])
 
     def body(asks, order):
         if not asks:
@@ -365,7 +445,7 @@
             back[:, : group * HD] = dq_sib_in[...]
             back[:, group * HD :] = near_sib_in[...].astype(low)
             return
-        near, keys, _ = head_parts(asks, order, own_all, sib_all, far, key_at, value_at)
+        queries, grads, keys, _ = head_parts(asks, order, own_all, sib_all, far, unit["head"])
         keys_t = keys.T
         distant = 2 * rows
         dk, dv, told = [None, None], [None, None], [None, None]
@@ -373,8 +453,7 @@
             for side in range(2):
                 slot = pair * 2 + side
                 count = distant + (side + 1) * rows
-                q = stacked(near[side], query_at, pair)
-                g = stacked(near[side], grad_at, pair)
+                q, g = queries(side, pair), grads(side, pair)
                 probs, score_grad = probs_in[slot, :count], grads_in[slot, :count]
                 wanted = order(0, rows)[1]
                 accumulate(told, 0, contract(score_grad[wanted : wanted + rows], q, 1, 0))
@@ -408,14 +487,14 @@
         back[:, index * width : (index + 1) * width] = (nears[index][...] + told).astype(back.dtype)
 
 
-def join_kernel(units, place, *refs):
+def join_kernel(plan, place, *refs):
     outs, (sums, sems) = refs[-5:-2], refs[-2:]
     core = place[0] % 2
     hears = place[0] // 2 == 0
     group = QH // KVH
     halves = [out.shape[1] // 2 for out in outs]
-    amount = len(units)
-    late = units[0]["told"] == 2
+    rows = sums.shape[1]
+    own_rows = pl.multiple_of(core * rows, HD)
     copies = []
 
     def write(source, out, start, width):
@@ -423,36 +502,30 @@
         copies.append(pltpu.make_async_copy(source, target, sems.at[len(copies)]))
         copies[-1].start()
 
-    for index, unit in enumerate(units):
+    def write_pair(source, at, head, owner):
+        for slot in range(2):
+            spot = slice(at + slot * HD, at + (slot + 1) * HD)
+            write(source.at[:, spot], outs[1 + slot], owner * halves[1] + head * HD, HD)
+
+    for head, own, other in plan["queries"]:
         width = group * HD
-        at = unit["head"] * width
-        sib_part = refs[amount + index]
-        write(refs[index], outs[0], core * halves[0] + at, width)
-        write(sib_part.at[:, :width], outs[0], (1 - core) * halves[0] + at, width)
-    own_rows = pl.multiple_of(core * refs[0].shape[0], HD)
-    for index, unit in enumerate(units):
-        near, told = refs[2 * amount + index], refs[3 * amount + index]
-        rows = near.shape[0]
-        heard = told[...] if late else told[pl.ds(own_rows, rows), :]
-        total = near[...] + jnp.where(hears, heard.astype(jnp.float32), 0.0)
-        sums[index] = total.astype(sums.dtype)
-        for slot in range(2):
-            start = core * halves[1] + unit["head"] * HD
-            write(sums.at[index, :, slot * HD : (slot + 1) * HD], outs[1 + slot], start, HD)
-    other = refs[4 * amount]
-    if late:
-        told = refs[4 * amount + 1]
-        rows = told.shape[0]
-        total = other[:, group * HD :].astype(jnp.float32) + jnp.where(
-            hears, told[...].astype(jnp.float32), 0.0
-        )
-        sums[amount] = total.astype(sums.dtype)
-        other = sums.at[amount]
-    for index, unit in enumerate(units):
-        for slot in range(2):
-            start = (1 - core) * halves[1] + unit["head"] * HD
-            at = (2 * index + slot) * HD
-            write(other.at[:, at : at + HD], outs[1 + slot], start, HD)
+        write(refs[own], outs[0], core * halves[0] + head * width, width)
+        write(refs[other].at[:, :width], outs[0], (1 - core) * halves[0] + head * width, width)
+    for head, other, at in plan["ready"]:
+        write_pair(refs[other], at, head, 1 - core)
+    cell = 0
+    for head, near, told, direct in plan["own"]:
+        heard = refs[told][...] if direct else refs[told][pl.ds(own_rows, rows), :]
+        total = refs[near][...] + jnp.where(hears, heard.astype(jnp.float32), 0.0)
+        sums[cell] = total.astype(sums.dtype)
+        write_pair(sums.at[cell], 0, head, core)
+        cell += 1
+    for head, other, at, told in plan["other"]:
+        total = refs[other][:, at : at + 2 * HD].astype(jnp.float32)
+        total = total + jnp.where(hears, refs[told][...].astype(jnp.float32), 0.0)
+        sums[cell] = total.astype(sums.dtype)
+        write_pair(sums.at[cell], 0, head, 1 - core)
+        cell += 1
     for copy in copies:
         copy.wait()
 
@@ -506,33 +579,42 @@
     place = lax.axis_index("sp").astype(jnp.int32).reshape(1)
     whole = (query_rows, out_grad, key_rows, value_rows, question_lengths)
     fixed = tuple(pltpu.with_memory_space_constraint(value, pltpu.HBM) for value in whole)
-    *packs, sib_send = local_call(
-        pack_kernel, [link] * (2 * LAG) + [wide], (place, *fixed[:4]), space=pltpu.HBM,
-        scratch=[pltpu.SemaphoreType.DMA((4 * LAG + 4,))],
+    narrow = shape((rows, 2 * (group + 1) * HD), low)
+    lent = [wide, narrow, shape((2 * rows, 2 * rows), full)]
+    *packs, sib_send, own_first, bias = local_call(
+        pack_kernel, [link] * (2 * LAG) + lent, (place, *fixed[:4]), space=pltpu.HBM,
+        scratch=[pltpu.SemaphoreType.DMA((4 * LAG + 8,))],
+    )
+    args = (place, *fixed, sib_send, own_first, bias)
+    sib_send, own_first, bias = local_call(
+        lend_kernel, lent, args, aliases={6 + i: i for i in range(3)},
+        in_spaces=[pltpu.HBM] * 5 + [pltpu.VMEM] * 3,
+        scratch=[
+            pltpu.SMEM(question_lengths.shape, jnp.int32), pltpu.SemaphoreType.DMA((9,)),
+        ],
     )
     far = []
     for chunk in range(LAG):
         far.append((send(packs[2 * chunk], same), send(packs[2 * chunk + 1], cross)))
     sib_all = send(sib_send, sib)
-    own_all, bias = local_call(
-        stage_kernel, [wide, shape((2 * rows, 2 * rows), full)], (place, *fixed),
-        space=pltpu.HBM,
-        scratch=[
-            pltpu.SMEM(question_lengths.shape, jnp.int32), pltpu.SemaphoreType.DMA((5,)),
-        ],
-    )
     wings = [shape((rows, group * HD), low)] * 2
     near = shape((rows, 2 * HD), full)
     dq_own, dq_sib, near_own, near_sib = [], [], [], []
     for index, unit in enumerate(units):
         split = unit["told"] == 2
+        lead = index == 0
+        args = (place, bias, own_first if lead else own_all, sib_all, *far[index])
         outs = local_call(
             partial(attend_kernel, unit),
             [*wings, near, near, link if split else shape((2 * rows, 2 * HD), low)]
-            + ([block, block] if split else []),
-            (place, bias, own_all, sib_all, *far[index]),
+            + ([block, block] if split else []) + ([wide] if lead else []),
+            args + (fixed[:4] if lead else ()),
+            in_spaces=[pltpu.VMEM] * (len(args) - 1) + [pltpu.HBM] * (4 if lead else 0),
+            scratch=[pltpu.SemaphoreType.DMA((4,))] if lead else (),
             flops=group * 10 * HD * 2 * rows * 4 * rows,
         )
+        if lead:
+            own_all = outs[5]
         told = send(outs[4], same)
         if split:
             outs = local_call(
@@ -551,29 +633,50 @@
             near_own.append(outs[2])
             near_sib.append(outs[3])
     heard = [value[0] for value in far[LAG:]]
-    back_keys, = local_call(
-        partial(fold_kernel, count - 1), [shape((rows, (count - 1) * 2 * HD), low)],
-        (place, *near_sib, *heard),
-    )
-    back_keys = send(back_keys, sib)
     shapes = [shape(value.shape, low) for value in (query_rows, key_rows, value_rows)]
-
-    def join(part, args, results):
-        spaces = [pltpu.VMEM] * len(args) + [pltpu.HBM] * len(results)
+    ready, head = [], 0
+    for size in FOLDS:
+        span = slice(head, head + size)
+        folded, = local_call(
+            partial(fold_kernel, size), [shape((rows, size * 2 * HD), low)],
+            (place, *near_sib[span], *heard[span]),
+        )
+        folded = send(folded, sib)
+        ready.append([(head + i, folded, 2 * i * HD) for i in range(size)])
+        head += size
+
+    def join(results, queries, own, ready, other):
+        args = []
+
+        def use(value):
+            args.append(value)
+            return len(args) - 1
+
+        plan = {
+            "queries": [(at, use(first), use(second)) for at, first, second in queries],
+            "ready": [(at, use(value), spot) for at, value, spot in ready],
+            "own": [(at, use(near), use(told), direct) for at, near, told, direct in own],
+            "other": [(at, use(value), spot, use(told)) for at, value, spot, told in other],
+        }
+        cells = len(own) + len(other)
+        writes = 2 * (len(queries) + len(ready) + cells)
         return local_call(
-            partial(join_kernel, part), shapes, (place, *args, *results),
+            partial(join_kernel, plan), shapes, (place, *args, *results),
             aliases={1 + len(args) + i: i for i in range(len(results))},
-            in_spaces=spaces, out_space=pltpu.HBM,
-            scratch=[
-                pltpu.VMEM((len(part) + 1, rows, 2 * HD), low),
-                pltpu.SemaphoreType.DMA((6 * len(part),)),
-            ],
+            in_spaces=[pltpu.VMEM] * len(args) + [pltpu.HBM] * len(results),
+            out_space=pltpu.HBM,
+            scratch=[pltpu.VMEM((cells, rows, 2 * HD), low), pltpu.SemaphoreType.DMA((writes,))],
         )
 
-    results = join(units[:-1], (*dq_own, *dq_sib, *near_own, *heard, back_keys), ())
+    last = count - 1
+    queries = [(i, dq_own[i], dq_sib[i]) for i in range(last)]
+    own = [(i, near_own[i], heard[i], False) for i in range(last)]
+    soon = sum(FOLDS[:-1])
+    results = join((), queries, own[:soon], [item for part in ready[:-1] for item in part], ())
     results = join(
-        units[-1:], (dq_last, back_last, near_last, told_last, back_last, told_cross),
-        results,
+        results, [(last, dq_last, back_last)],
+        own[soon:] + [(last, near_last, told_last, True)], ready[-1],
+        [(last, back_last, group * HD, told_cross)],
     )
     return tuple(results)
 

time: 39 us -> 35.3 us (0.905)
  Pallas kernels: 11.8 us -> 8.29 us
  waiting for transfers between devices: 12.9 us -> 10.2 us
  starting transfers between devices: 13.2 us -> 15.7 us
    pallas_call x10 -> x11, Pallas kernels: 11.8 us -> 8.29 us  [local_call(): pl.pallas_call(kernel, out_shape=tuple(outs), in_specs=specs, out_specs=t...]
    ppermute x15 -> x18, waiting for transfers between devices: 12.9 us -> 10.2 us  [send(): return lax.ppermute(value, 'sp', perm)]
    ppermute x15 -> x18, starting transfers between devices: 13.2 us -> 15.7 us  [send(): return lax.ppermute(value, 'sp', perm)]
  transfers between devices with their start and end apart: 15 -> 18, of which waited for: 8 -> 7; matrix products, arithmetic and copies ran while one was open for 0% -> 0% of each run, Pallas kernels for 20% -> 16%
where the time goes in v2:
time: 35.3 us; the launch traced here: 35.1 us
  starting transfers between devices  15.7 us (44%)
  waiting for transfers between devices  10.2 us (29%)
  Pallas kernels  8.29 us (23%)
  between operations  0.91 us (3%)
    ppermute x18, starting transfers between devices, send(): return lax.ppermute(value, 'sp', perm)  15.7 us
    ppermute x18, waiting for transfers between devices, send(): return lax.ppermute(value, 'sp', perm)  10.2 us
    pallas_call x11, Pallas kernels, local_call(): pl.pallas_call(kernel, out_shape=tuple(outs), in_specs=specs, out_specs=t...  8.29 us
  transfers between devices with their start and end apart: 18, of which 7 were waited for; matrix products, arithmetic and copies ran while one was open for 0% of the time, Pallas kernels for 16%

profile of v2, /device:TPU:0, one launch (start us, length us, event | category | flops | bytes accessed | tf_op | source)
XLA Modules:
  0.0 35.1 jit_solution(1767349426951549057)
XLA Ops:
  0.6 1.8 %shard_map.76 = (bf16[128,256]{1,0:T(8,128)(2,1)S(1)}, bf16[128,256]{1,0:T(8,128)(2,1)S(1)}, bf16[128,256]{1,0:T(8,128)(2,1)S(1)}, bf16[128,256]{1,0:T(8,128)(2,...) custom-call(s32[1]{0:T(128)} %bitcast.place, ...), custom_call_target="tpu_custom_call" | custom-call | tf_op jit(solution)/shard_map/pallas_call | solution.py:536
  2.5 0.6 %collective-permute-start = (bf16[128,5120]{1,0:T(8,128)(2,1)S(1)}, bf16[128,5120]{1,0:T(8,128)(2,1)S(1)}, u32[]{:S(2)}, u32[]{:S(2)}) collective-permute-start(bf16[128,5120]{1,0:T(8,128)(2,1)S(1)} %get-tuple-element.50), channel_id=1, source_target_pairs={{0,1},{1,0},{2,3},{3,2},{4,5},{5,4},{6,7},{7,6},{8,9},{9,8},{10,11... | collective-permute-start | bytes 3932168 | tf_op jit(solution)/shard_map/ppermute | solution.py:577
  3.1 2.4 %collective-permute-start.1 = (bf16[128,256]{1,0:T(8,128)(2,1)S(1)}, bf16[128,256]{1,0:T(8,128)(2,1)S(1)}, u32[]{:S(2)}, u32[]{:S(2)}) collective-permute-start(bf16[128,256]{1,0:T(8,128)(2,1)S(1)} %get-tuple-element.51), channel_id=1, source_target_pairs={{0,2},{1,3},{2,0},{3,1},{4,6},{5,7},{6,4},{7,5},{8,10},{9,11},{10,... | collective-permute-start | bytes 196616 | tf_op jit(solution)/shard_map/ppermute | solution.py:577
  5.5 1.7 %collective-permute-start.12 = (bf16[128,256]{1,0:T(8,128)(2,1)S(1)}, bf16[128,256]{1,0:T(8,128)(2,1)S(1)}, u32[]{:S(2)}, u32[]{:S(2)}) collective-permute-start(bf16[128,256]{1,0:T(8,128)(2,1)S(1)} %get-tuple-element.73), channel_id=1, source_target_pairs={{0,2},{1,3},{2,0},{3,1},{4,6},{5,7},{6,4},{7,5},{8,10},{9,11},{10,... | collective-permute-start | bytes 196616 | tf_op jit(solution)/shard_map/ppermute | solution.py:577
  7.2 0.9 %collective-permute-done.1.refs_0_ = bf16[128,256]{1,0:T(8,128)(2,1)S(1)} collective-permute-done((bf16[128,256]{1,0:T(8,128)(2,1)S(1)}, bf16[128,256]{1,0:T(8,128)(2,1)S(1)}, u32[]{:S(2)}, u32[]{:S(2)}) %collective-permute-start.1) | collective-permute-done | bytes 65568 | tf_op jit(solution)/shard_map/ppermute | solution.py:577
  8.1 1.4 %collective-permute-done.2.refs_1_ = bf16[128,256]{1,0:T(8,128)(2,1)S(1)} collective-permute-done((bf16[128,256]{1,0:T(8,128)(2,1)S(1)}, bf16[128,256]{1,0:T(8,128)(2,1)S(1)}, u32[]{:S(2)}, u32[]{:S(2)}) %collective-permute-start.2) | collective-permute-done | bytes 65568 | tf_op jit(solution)/shard_map/ppermute | solution.py:577
  9.5 1.3 %shard_map.78 = (bf16[128,512]{1,0:T(8,128)(2,1)S(1)}, bf16[128,512]{1,0:T(8,128)(2,1)S(1)}, f32[128,256]{1,0:T(8,128)S(1)}, f32[128,256]{1,0:T(8,128)S(1)}, bf1...) custom-call(s32[1]{0:T(128)} %bitcast.place, f32[256,256]{1,0:T(8,128)S(1)} %get-tuple-element.48.bias, ...), custom_call_target="tpu_custom_call" | custom-call | flops 671088640 | tf_op jit(solution)/shard_map/pallas_call | solution.py:536
  10.8 1.9 %collective-permute-start.3 = (bf16[256,256]{1,0:T(8,128)(2,1)S(1)}, bf16[256,256]{1,0:T(8,128)(2,1)S(1)}, u32[]{:S(2)}, u32[]{:S(2)}) collective-permute-start(bf16[256,256]{1,0:T(8,128)(2,1)S(1)} %get-tuple-element.54), channel_id=1, source_target_pairs={{0,2},{1,3},{2,0},{3,1},{4,6},{5,7},{6,4},{7,5},{8,10},{9,11},{10,... | collective-permute-start | bytes 393224 | tf_op jit(solution)/shard_map/ppermute | solution.py:577
  12.9 1.7 %collective-permute-start.6 = (bf16[128,256]{1,0:T(8,128)(2,1)S(1)}, bf16[128,256]{1,0:T(8,128)(2,1)S(1)}, u32[]{:S(2)}, u32[]{:S(2)}) collective-permute-start(bf16[128,256]{1,0:T(8,128)(2,1)S(1)} %get-tuple-element.64), channel_id=1, source_target_pairs={{0,3},{1,2},{2,1},{3,0},{4,7},{5,6},{6,5},{7,4},{8,11},{9,10},{10,... | collective-permute-start | bytes 196616 | tf_op jit(solution)/shard_map/ppermute | solution.py:577
  14.7 1.0 %shard_map.83 = (bf16[128,512]{1,0:T(8,128)(2,1)S(1)}, bf16[128,512]{1,0:T(8,128)(2,1)S(1)}, f32[128,256]{1,0:T(8,128)S(1)}, f32[128,256]{1,0:T(8,128)S(1)}, bf16[256,256]{1,0:T(8,128)(2,1)S(1)}) custom-call(s32[1]{0:T(128)} %bitcast.place, f32[256,256]{1,0:T(8,128)S(1)} %get-tuple-element.48.bias, bf16[128,5120]{1,0:T(8,128)(2,1)S(1)} %get-tuple-element.53.own_all, ...), custom_call_target="tpu_custom_call" | custom-call | flops 671088640 | tf_op jit(solution)/shard_map/pallas_call | solution.py:536
  15.7 1.3 %collective-permute-start.16 = (bf16[256,256]{1,0:T(8,128)(2,1)S(1)}, bf16[256,256]{1,0:T(8,128)(2,1)S(1)}, u32[]{:S(2)}, u32[]{:S(2)}) collective-permute-start(bf16[256,256]{1,0:T(8,128)(2,1)S(1)} %get-tuple-element.81), channel_id=1, source_target_pairs={{0,2},{1,3},{2,0},{3,1},{4,6},{5,7},{6,4},{7,5},{8,10},{9,11},{10,... | collective-permute-start | bytes 393224 | tf_op jit(solution)/shard_map/ppermute | solution.py:577
  16.9 1.7 %collective-permute-done.5.refs_0_ = bf16[128,256]{1,0:T(8,128)(2,1)S(1)} collective-permute-done((bf16[128,256]{1,0:T(8,128)(2,1)S(1)}, bf16[128,256]{1,0:T(8,128)(2,1)S(1)}, u32[]{:S(2)}, u32[]{:S(2)}) %collective-permute-start.5) | collective-permute-done | bytes 65568 | tf_op jit(solution)/shard_map/ppermute | solution.py:577
  18.7 1.4 %collective-permute-done.6.refs_1_ = bf16[128,256]{1,0:T(8,128)(2,1)S(1)} collective-permute-done((bf16[128,256]{1,0:T(8,128)(2,1)S(1)}, bf16[128,256]{1,0:T(8,128)(2,1)S(1)}, u32[]{:S(2)}, u32[]{:S(2)}) %collective-permute-start.6) | collective-permute-done | bytes 65568 | tf_op jit(solution)/shard_map/ppermute | solution.py:577
  20.0 1.0 %shard_map.81 = (bf16[128,512]{1,0:T(8,128)(2,1)S(1)}, bf16[128,512]{1,0:T(8,128)(2,1)S(1)}, f32[128,256]{1,0:T(8,128)S(1)}, f32[128,256]{1,0:T(8,128)S(1)}, bf16[256,256]{1,0:T(8,128)(2,1)S(1)}) custom-call(s32[1]{0:T(128)} %bitcast.place, f32[256,256]{1,0:T(8,128)S(1)} %get-tuple-element.48.bias, bf16[128,5120]{1,0:T(8,128)(2,1)S(1)} %get-tuple-element.53.own_all, ...), custom_call_target="tpu_custom_call" | custom-call | flops 671088640 | tf_op jit(solution)/shard_map/pallas_call | solution.py:536
  21.1 2.5 %collective-permute-start.7 = (bf16[256,256]{1,0:T(8,128)(2,1)S(1)}, bf16[256,256]{1,0:T(8,128)(2,1)S(1)}, u32[]{:S(2)}, u32[]{:S(2)}) collective-permute-start(bf16[256,256]{1,0:T(8,128)(2,1)S(1)} %get-tuple-element.66), channel_id=1, source_target_pairs={{0,2},{1,3},{2,0},{3,1},{4,6},{5,7},{6,4},{7,5},{8,10},{9,11},{10,... | collective-permute-start | bytes 393224 | tf_op jit(solution)/shard_map/ppermute | solution.py:577
  24.1 1.0 %shard_map.79 = (bf16[128,512]{1,0:T(8,128)(2,1)S(1)}, bf16[128,512]{1,0:T(8,128)(2,1)S(1)}, f32[128,256]{1,0:T(8,128)S(1)}, f32[128,256]{1,0:T(8,128)S(1)}, bf1...) custom-call(s32[1]{0:T(128)} %bitcast.place, ...), custom_call_target="tpu_custom_call" | custom-call | flops 671088640 | tf_op jit(solution)/shard_map/pallas_call | solution.py:536
  25.2 0.6 %collective-permute-start.4 = (bf16[128,768]{1,0:T(8,128)(2,1)S(1)}, bf16[128,768]{1,0:T(8,128)(2,1)S(1)}, u32[]{:S(2)}, u32[]{:S(2)}) collective-permute-start(bf16[128,768]{1,0:T(8,128)(2,1)S(1)} %get-tuple-element.62), channel_id=1, source_target_pairs={{0,1},{1,0},{2,3},{3,2},{4,5},{5,4},{6,7},{7,6},{8,9},{9,8},{10,11... | collective-permute-start | bytes 589832 | tf_op jit(solution)/shard_map/ppermute | solution.py:577
  25.8 1.5 %collective-permute-done.7.refs_1_.refs_4_ = bf16[256,256]{1,0:T(8,128)(2,1)S(1)} collective-permute-done((bf16[256,256]{1,0:T(8,128)(2,1)S(1)}, bf16[256,256]{1,0:T(8,128)(2,1)S(1)}, u32[]{:S(2)}, u32[]{:S(2)}) %collective-permute-start.7) | collective-permute-done | bytes 131104 | tf_op jit(solution)/shard_map/ppermute | solution.py:577
  27.4 0.6 %collective-permute-start.8 = (bf16[128,256]{1,0:T(8,128)(2,1)S(1)}, bf16[128,256]{1,0:T(8,128)(2,1)S(1)}, u32[]{:S(2)}, u32[]{:S(2)}) collective-permute-start(bf16[128,256]{1,0:T(8,128)(2,1)S(1)} %shard_map.82), channel_id=1, source_target_pairs={{0,1},{1,0},{2,3},{3,2},{4,5},{5,4},{6,7},{7,6},{8,9},{9,8},{10,11... | collective-permute-start | bytes 196616 | tf_op jit(solution)/shard_map/ppermute | solution.py:577
  28.0 1.7 %collective-permute-start.9 = (bf16[128,256]{1,0:T(8,128)(2,1)S(1)}, bf16[128,256]{1,0:T(8,128)(2,1)S(1)}, u32[]{:S(2)}, u32[]{:S(2)}) collective-permute-start(bf16[128,256]{1,0:T(8,128)(2,1)S(1)} %get-tuple-element.69), channel_id=1, source_target_pairs={{0,2},{1,3},{2,0},{3,1},{4,6},{5,7},{6,4},{7,5},{8,10},{9,11},{10,... | collective-permute-start | bytes 196616 | tf_op jit(solution)/shard_map/ppermute | solution.py:577
  29.7 1.1 %shard_map.85 = (bf16[128,4096]{1,0:T(8,128)(2,1)}, bf16[128,1024]{1,0:T(8,128)(2,1)}, bf16[128,1024]{1,0:T(8,128)(2,1)}) custom-call(s32[1]{0:T(128)} %bitcast.place, bf16[128,512]{1,0:T(8,128)(2,1)S(1)} %get-tuple-element.71.refs_0_, bf16[128,512]{1,0:T(8,128)(2,1)S(1)} %collective-permute-done.11.refs_1_, bf16[128,512]{1,0:T(8,128)(2,1)S(1)} %get-tuple-element.75.refs_2_, ...), custom_call_target="tpu_custom_call" | custom-call | tf_op jit(solution)/shard_map/pallas_call | solution.py:536
  30.8 1.4 %collective-permute-done.9.refs_6_ = bf16[128,256]{1,0:T(8,128)(2,1)S(1)} collective-permute-done((bf16[128,256]{1,0:T(8,128)(2,1)S(1)}, bf16[128,256]{1,0:T(8,128)(2,1)S(1)}, u32[]{:S(2)}, u32[]{:S(2)}) %collective-permute-start.9) | collective-permute-done | bytes 65568 | tf_op jit(solution)/shard_map/ppermute | solution.py:577
  32.2 1.9 %collective-permute-done.10.refs_8_ = bf16[128,256]{1,0:T(8,128)(2,1)S(1)} collective-permute-done((bf16[128,256]{1,0:T(8,128)(2,1)S(1)}, bf16[128,256]{1,0:T(8,128)(2,1)S(1)}, u32[]{:S(2)}, u32[]{:S(2)}) %collective-permute-start.10) | collective-permute-done | bytes 65568 | tf_op jit(solution)/shard_map/ppermute | solution.py:577
  34.1 0.9 %shard_map.86 = (bf16[128,4096]{1,0:T(8,128)(2,1)}, bf16[128,1024]{1,0:T(8,128)(2,1)}, bf16[128,1024]{1,0:T(8,128)(2,1)}) custom-call(s32[1]{0:T(128)} %bitcast.place, bf16[128,512]{1,0:T(8,128)(2,1)S(1)} %get-tuple-element.61.refs_0_, ...), custom_call_target="tpu_custom_call", output_to_operand_aliasing={{0}: (10, {}), {1}: (11, {}), {2}: (12, {})} | custom-call | tf_op jit(solution)/shard_map/pallas_call | solution.py:536
  (23 shorter events, 1.0 us)
Async XLA Ops:
  2.5 7.0 %collective-permute-start = (bf16[128,5120]{1,0:T(8,128)(2,1)S(1)}, bf16[128,5120]{1,0:T(8,128)(2,1)S(1)}, u32[]{:S(2)}, u32[]{:S(2)}) collective-permute-start(bf16[128,5120]{1,0:T(8,128)(2,1)S(1)} %get-tuple-element.50), channel_id=1, source_target_pairs={{0,1},{1,0},{2,3},{3,2},{4,5},{5,4},{6,7},{7,6},{8,9},{9,8},{10,11... | collective-permute-start | bytes 3932168 | tf_op jit(solution)/shard_map/ppermute | solution.py:577
  3.1 5.0 %collective-permute-start.1 = (bf16[128,256]{1,0:T(8,128)(2,1)S(1)}, bf16[128,256]{1,0:T(8,128)(2,1)S(1)}, u32[]{:S(2)}, u32[]{:S(2)}) collective-permute-start(bf16[128,256]{1,0:T(8,128)(2,1)S(1)} %get-tuple-element.51), channel_id=1, source_target_pairs={{0,2},{1,3},{2,0},{3,1},{4,6},{5,7},{6,4},{7,5},{8,10},{9,11},{10,... | collective-permute-start | bytes 196616 | tf_op jit(solution)/shard_map/ppermute | solution.py:577
  5.4 4.1 %collective-permute-start.2 = (bf16[128,256]{1,0:T(8,128)(2,1)S(1)}, bf16[128,256]{1,0:T(8,128)(2,1)S(1)}, u32[]{:S(2)}, u32[]{:S(2)}) collective-permute-start(bf16[128,256]{1,0:T(8,128)(2,1)S(1)} %get-tuple-element.52), channel_id=1, source_target_pairs={{0,3},{1,2},{2,1},{3,0},{4,7},{5,6},{6,5},{7,4},{8,11},{9,10},{10,... | collective-permute-start | bytes 196616 | tf_op jit(solution)/shard_map/ppermute | solution.py:577
  5.5 9.2 %collective-permute-start.12 = (bf16[128,256]{1,0:T(8,128)(2,1)S(1)}, bf16[128,256]{1,0:T(8,128)(2,1)S(1)}, u32[]{:S(2)}, u32[]{:S(2)}) collective-permute-start(bf16[128,256]{1,0:T(8,128)(2,1)S(1)} %get-tuple-element.73), channel_id=1, source_target_pairs={{0,2},{1,3},{2,0},{3,1},{4,6},{5,7},{6,4},{7,5},{8,10},{9,11},{10,... | collective-permute-start | bytes 196616 | tf_op jit(solution)/shard_map/ppermute | solution.py:577
  7.2 7.4 %collective-permute-start.13 = (bf16[128,256]{1,0:T(8,128)(2,1)S(1)}, bf16[128,256]{1,0:T(8,128)(2,1)S(1)}, u32[]{:S(2)}, u32[]{:S(2)}) collective-permute-start(bf16[128,256]{1,0:T(8,128)(2,1)S(1)} %get-tuple-element.74), channel_id=1, source_target_pairs={{0,3},{1,2},{2,1},{3,0},{4,7},{5,6},{6,5},{7,4},{8,11},{9,10},{10,... | collective-permute-start | bytes 196616 | tf_op jit(solution)/shard_map/ppermute | solution.py:577
  10.8 13.3 %collective-permute-start.3 = (bf16[256,256]{1,0:T(8,128)(2,1)S(1)}, bf16[256,256]{1,0:T(8,128)(2,1)S(1)}, u32[]{:S(2)}, u32[]{:S(2)}) collective-permute-start(bf16[256,256]{1,0:T(8,128)(2,1)S(1)} %get-tuple-element.54), channel_id=1, source_target_pairs={{0,2},{1,3},{2,0},{3,1},{4,6},{5,7},{6,4},{7,5},{8,10},{9,11},{10,... | collective-permute-start | bytes 393224 | tf_op jit(solution)/shard_map/ppermute | solution.py:577
  12.7 6.0 %collective-permute-start.5 = (bf16[128,256]{1,0:T(8,128)(2,1)S(1)}, bf16[128,256]{1,0:T(8,128)(2,1)S(1)}, u32[]{:S(2)}, u32[]{:S(2)}) collective-permute-start(bf16[128,256]{1,0:T(8,128)(2,1)S(1)} %get-tuple-element.63), channel_id=1, source_target_pairs={{0,2},{1,3},{2,0},{3,1},{4,6},{5,7},{6,4},{7,5},{8,10},{9,11},{10,... | collective-permute-start | bytes 196616 | tf_op jit(solution)/shard_map/ppermute | solution.py:577
  12.9 7.1 %collective-permute-start.6 = (bf16[128,256]{1,0:T(8,128)(2,1)S(1)}, bf16[128,256]{1,0:T(8,128)(2,1)S(1)}, u32[]{:S(2)}, u32[]{:S(2)}) collective-permute-start(bf16[128,256]{1,0:T(8,128)(2,1)S(1)} %get-tuple-element.64), channel_id=1, source_target_pairs={{0,3},{1,2},{2,1},{3,0},{4,7},{5,6},{6,5},{7,4},{8,11},{9,10},{10,... | collective-permute-start | bytes 196616 | tf_op jit(solution)/shard_map/ppermute | solution.py:577
  15.7 9.5 %collective-permute-start.16 = (bf16[256,256]{1,0:T(8,128)(2,1)S(1)}, bf16[256,256]{1,0:T(8,128)(2,1)S(1)}, u32[]{:S(2)}, u32[]{:S(2)}) collective-permute-start(bf16[256,256]{1,0:T(8,128)(2,1)S(1)} %get-tuple-element.81), channel_id=1, source_target_pairs={{0,2},{1,3},{2,0},{3,1},{4,6},{5,7},{6,4},{7,5},{8,10},{9,11},{10,... | collective-permute-start | bytes 393224 | tf_op jit(solution)/shard_map/ppermute | solution.py:577
  21.1 6.3 %collective-permute-start.7 = (bf16[256,256]{1,0:T(8,128)(2,1)S(1)}, bf16[256,256]{1,0:T(8,128)(2,1)S(1)}, u32[]{:S(2)}, u32[]{:S(2)}) collective-permute-start(bf16[256,256]{1,0:T(8,128)(2,1)S(1)} %get-tuple-element.66), channel_id=1, source_target_pairs={{0,2},{1,3},{2,0},{3,1},{4,6},{5,7},{6,4},{7,5},{8,10},{9,11},{10,... | collective-permute-start | bytes 393224 | tf_op jit(solution)/shard_map/ppermute | solution.py:577
  23.6 3.8 %collective-permute-start.11 = (bf16[128,512]{1,0:T(8,128)(2,1)S(1)}, bf16[128,512]{1,0:T(8,128)(2,1)S(1)}, u32[]{:S(2)}, u32[]{:S(2)}) collective-permute-start(bf16[128,512]{1,0:T(8,128)(2,1)S(1)} %get-tuple-element.72), channel_id=1, source_target_pairs={{0,1},{1,0},{2,3},{3,2},{4,5},{5,4},{6,7},{7,6},{8,9},{9,8},{10,11... | collective-permute-start | bytes 393224 | tf_op jit(solution)/shard_map/ppermute | solution.py:577
  23.6 4.4 %collective-permute-start.14 = (bf16[128,512]{1,0:T(8,128)(2,1)S(1)}, bf16[128,512]{1,0:T(8,128)(2,1)S(1)}, u32[]{:S(2)}, u32[]{:S(2)}) collective-permute-start(bf16[128,512]{1,0:T(8,128)(2,1)S(1)} %get-tuple-element.76), channel_id=1, source_target_pairs={{0,1},{1,0},{2,3},{3,2},{4,5},{5,4},{6,7},{7,6},{8,9},{9,8},{10,11... | collective-permute-start | bytes 393224 | tf_op jit(solution)/shard_map/ppermute | solution.py:577
  24.1 5.6 %collective-permute-start.15 = (bf16[128,512]{1,0:T(8,128)(2,1)S(1)}, bf16[128,512]{1,0:T(8,128)(2,1)S(1)}, u32[]{:S(2)}, u32[]{:S(2)}) collective-permute-start(bf16[128,512]{1,0:T(8,128)(2,1)S(1)} %get-tuple-element.78), channel_id=1, source_target_pairs={{0,1},{1,0},{2,3},{3,2},{4,5},{5,4},{6,7},{7,6},{8,9},{9,8},{10,11... | collective-permute-start | bytes 393224 | tf_op jit(solution)/shard_map/ppermute | solution.py:577
  25.2 8.9 %collective-permute-start.4 = (bf16[128,768]{1,0:T(8,128)(2,1)S(1)}, bf16[128,768]{1,0:T(8,128)(2,1)S(1)}, u32[]{:S(2)}, u32[]{:S(2)}) collective-permute-start(bf16[128,768]{1,0:T(8,128)(2,1)S(1)} %get-tuple-element.62), channel_id=1, source_target_pairs={{0,1},{1,0},{2,3},{3,2},{4,5},{5,4},{6,7},{7,6},{8,9},{9,8},{10,11... | collective-permute-start | bytes 589832 | tf_op jit(solution)/shard_map/ppermute | solution.py:577
  27.4 2.4 %collective-permute-start.17 = (bf16[128,512]{1,0:T(8,128)(2,1)S(1)}, bf16[128,512]{1,0:T(8,128)(2,1)S(1)}, u32[]{:S(2)}, u32[]{:S(2)}) collective-permute-start(bf16[128,512]{1,0:T(8,128)(2,1)S(1)} %shard_map.84), channel_id=1, source_target_pairs={{0,1},{1,0},{2,3},{3,2},{4,5},{5,4},{6,7},{7,6},{8,9},{9,8},{10,11... | collective-permute-start | bytes 393224 | tf_op jit(solution)/shard_map/ppermute | solution.py:577
  27.4 3.4 %collective-permute-start.8 = (bf16[128,256]{1,0:T(8,128)(2,1)S(1)}, bf16[128,256]{1,0:T(8,128)(2,1)S(1)}, u32[]{:S(2)}, u32[]{:S(2)}) collective-permute-start(bf16[128,256]{1,0:T(8,128)(2,1)S(1)} %shard_map.82), channel_id=1, source_target_pairs={{0,1},{1,0},{2,3},{3,2},{4,5},{5,4},{6,7},{7,6},{8,9},{9,8},{10,11... | collective-permute-start | bytes 196616 | tf_op jit(solution)/shard_map/ppermute | solution.py:577
  28.0 4.3 %collective-permute-start.9 = (bf16[128,256]{1,0:T(8,128)(2,1)S(1)}, bf16[128,256]{1,0:T(8,128)(2,1)S(1)}, u32[]{:S(2)}, u32[]{:S(2)}) collective-permute-start(bf16[128,256]{1,0:T(8,128)(2,1)S(1)} %get-tuple-element.69), channel_id=1, source_target_pairs={{0,2},{1,3},{2,0},{3,1},{4,6},{5,7},{6,4},{7,5},{8,10},{9,11},{10,... | collective-permute-start | bytes 196616 | tf_op jit(solution)/shard_map/ppermute | solution.py:577
  29.7 4.4 %collective-permute-start.10 = (bf16[128,256]{1,0:T(8,128)(2,1)S(1)}, bf16[128,256]{1,0:T(8,128)(2,1)S(1)}, u32[]{:S(2)}, u32[]{:S(2)}) collective-permute-start(bf16[128,256]{1,0:T(8,128)(2,1)S(1)} %get-tuple-element.70), channel_id=1, source_target_pairs={{0,3},{1,2},{2,1},{3,0},{4,7},{5,6},{6,5},{7,4},{8,11},{9,10},{10,... | collective-permute-start | bytes 196616 | tf_op jit(solution)/shard_map/ppermute | solution.py:577

commit v3 on v2

--- a/solution.py
+++ b/solution.py
@@ -672,9 +672,11 @@
     queries = [(i, dq_own[i], dq_sib[i]) for i in range(last)]
     own = [(i, near_own[i], heard[i], False) for i in range(last)]
     soon = sum(FOLDS[:-1])
-    results = join((), queries, own[:soon], [item for part in ready[:-1] for item in part], ())
     results = join(
-        results, [(last, dq_last, back_last)],
+        (), queries + [(last, dq_last, back_last)], own[:soon], [item for part in ready[:-1] for item in part], ()
+    )
+    results = join(
+        results, (),
         own[soon:] + [(last, near_last, told_last, True)], ready[-1],
         [(last, back_last, group * HD, told_cross)],
     )

time: 35.3 us -> 34.7 us (0.983)
  waiting for transfers between devices: 10.2 us -> 9.71 us
    ppermute x18, waiting for transfers between devices: 10.2 us -> 9.71 us  [send(): return lax.ppermute(value, 'sp', perm)]
where the time goes in v3:
time: 34.7 us; the launch traced here: 34.5 us
  starting transfers between devices  15.6 us (45%)
  waiting for transfers between devices  9.71 us (28%)
  Pallas kernels  8.3 us (24%)
  between operations  0.91 us (3%)
    ppermute x18, starting transfers between devices, send(): return lax.ppermute(value, 'sp', perm)  15.6 us
    ppermute x18, waiting for transfers between devices, send(): return lax.ppermute(value, 'sp', perm)  9.71 us
    pallas_call x11, Pallas kernels, local_call(): pl.pallas_call(kernel, out_shape=tuple(outs), in_specs=specs, out_specs=t...  8.3 us
  transfers between devices with their start and end apart: 18, of which 7 were waited for; matrix products, arithmetic and copies ran while one was open for 0% of the time, Pallas kernels for 16%

profile of v3, /device:TPU:0, one launch (start us, length us, event | category | flops | bytes accessed | tf_op | source)
XLA Modules:
  0.0 34.5 jit_solution(14323515199926965015)
XLA Ops:
  0.6 1.8 %shard_map.76 = (bf16[128,256]{1,0:T(8,128)(2,1)S(1)}, bf16[128,256]{1,0:T(8,128)(2,1)S(1)}, bf16[128,256]{1,0:T(8,128)(2,1)S(1)}, bf16[128,256]{1,0:T(8,128)(2,...) custom-call(s32[1]{0:T(128)} %bitcast.place, ...), custom_call_target="tpu_custom_call" | custom-call | tf_op jit(solution)/shard_map/pallas_call | solution.py:536
  2.5 0.6 %collective-permute-start = (bf16[128,5120]{1,0:T(8,128)(2,1)S(1)}, bf16[128,5120]{1,0:T(8,128)(2,1)S(1)}, u32[]{:S(2)}, u32[]{:S(2)}) collective-permute-start(bf16[128,5120]{1,0:T(8,128)(2,1)S(1)} %get-tuple-element.50), channel_id=1, source_target_pairs={{0,1},{1,0},{2,3},{3,2},{4,5},{5,4},{6,7},{7,6},{8,9},{9,8},{10,11... | collective-permute-start | bytes 3932168 | tf_op jit(solution)/shard_map/ppermute | solution.py:577
  3.1 2.4 %collective-permute-start.1 = (bf16[128,256]{1,0:T(8,128)(2,1)S(1)}, bf16[128,256]{1,0:T(8,128)(2,1)S(1)}, u32[]{:S(2)}, u32[]{:S(2)}) collective-permute-start(bf16[128,256]{1,0:T(8,128)(2,1)S(1)} %get-tuple-element.51), channel_id=1, source_target_pairs={{0,2},{1,3},{2,0},{3,1},{4,6},{5,7},{6,4},{7,5},{8,10},{9,11},{10,... | collective-permute-start | bytes 196616 | tf_op jit(solution)/shard_map/ppermute | solution.py:577
  5.5 1.7 %collective-permute-start.12 = (bf16[128,256]{1,0:T(8,128)(2,1)S(1)}, bf16[128,256]{1,0:T(8,128)(2,1)S(1)}, u32[]{:S(2)}, u32[]{:S(2)}) collective-permute-start(bf16[128,256]{1,0:T(8,128)(2,1)S(1)} %get-tuple-element.72), channel_id=1, source_target_pairs={{0,2},{1,3},{2,0},{3,1},{4,6},{5,7},{6,4},{7,5},{8,10},{9,11},{10,... | collective-permute-start | bytes 196616 | tf_op jit(solution)/shard_map/ppermute | solution.py:577
  7.2 0.9 %collective-permute-done.1.refs_0_ = bf16[128,256]{1,0:T(8,128)(2,1)S(1)} collective-permute-done((bf16[128,256]{1,0:T(8,128)(2,1)S(1)}, bf16[128,256]{1,0:T(8,128)(2,1)S(1)}, u32[]{:S(2)}, u32[]{:S(2)}) %collective-permute-start.1) | collective-permute-done | bytes 65568 | tf_op jit(solution)/shard_map/ppermute | solution.py:577
  8.1 1.4 %collective-permute-done.2.refs_1_ = bf16[128,256]{1,0:T(8,128)(2,1)S(1)} collective-permute-done((bf16[128,256]{1,0:T(8,128)(2,1)S(1)}, bf16[128,256]{1,0:T(8,128)(2,1)S(1)}, u32[]{:S(2)}, u32[]{:S(2)}) %collective-permute-start.2) | collective-permute-done | bytes 65568 | tf_op jit(solution)/shard_map/ppermute | solution.py:577
  9.5 1.3 %shard_map.78 = (bf16[128,512]{1,0:T(8,128)(2,1)S(1)}, bf16[128,512]{1,0:T(8,128)(2,1)S(1)}, f32[128,256]{1,0:T(8,128)S(1)}, f32[128,256]{1,0:T(8,128)S(1)}, bf1...) custom-call(s32[1]{0:T(128)} %bitcast.place, f32[256,256]{1,0:T(8,128)S(1)} %get-tuple-element.48.bias, ...), custom_call_target="tpu_custom_call" | custom-call | flops 671088640 | tf_op jit(solution)/shard_map/pallas_call | solution.py:536
  10.8 1.9 %collective-permute-start.7 = (bf16[256,256]{1,0:T(8,128)(2,1)S(1)}, bf16[256,256]{1,0:T(8,128)(2,1)S(1)}, u32[]{:S(2)}, u32[]{:S(2)}) collective-permute-start(bf16[256,256]{1,0:T(8,128)(2,1)S(1)} %get-tuple-element.59), channel_id=1, source_target_pairs={{0,2},{1,3},{2,0},{3,1},{4,6},{5,7},{6,4},{7,5},{8,10},{9,11},{10,... | collective-permute-start | bytes 393224 | tf_op jit(solution)/shard_map/ppermute | solution.py:577
  12.9 1.7 %collective-permute-start.4 = (bf16[128,256]{1,0:T(8,128)(2,1)S(1)}, bf16[128,256]{1,0:T(8,128)(2,1)S(1)}, u32[]{:S(2)}, u32[]{:S(2)}) collective-permute-start(bf16[128,256]{1,0:T(8,128)(2,1)S(1)} %get-tuple-element.55), channel_id=1, source_target_pairs={{0,3},{1,2},{2,1},{3,0},{4,7},{5,6},{6,5},{7,4},{8,11},{9,10},{10,... | collective-permute-start | bytes 196616 | tf_op jit(solution)/shard_map/ppermute | solution.py:577
  14.7 1.0 %shard_map.83 = (bf16[128,512]{1,0:T(8,128)(2,1)S(1)}, bf16[128,512]{1,0:T(8,128)(2,1)S(1)}, f32[128,256]{1,0:T(8,128)S(1)}, f32[128,256]{1,0:T(8,128)S(1)}, bf16[256,256]{1,0:T(8,128)(2,1)S(1)}) custom-call(s32[1]{0:T(128)} %bitcast.place, f32[256,256]{1,0:T(8,128)S(1)} %get-tuple-element.48.bias, bf16[128,5120]{1,0:T(8,128)(2,1)S(1)} %get-tuple-element.53.own_all, ...), custom_call_target="tpu_custom_call" | custom-call | flops 671088640 | tf_op jit(solution)/shard_map/pallas_call | solution.py:536
  15.7 1.3 %collective-permute-start.16 = (bf16[256,256]{1,0:T(8,128)(2,1)S(1)}, bf16[256,256]{1,0:T(8,128)(2,1)S(1)}, u32[]{:S(2)}, u32[]{:S(2)}) collective-permute-start(bf16[256,256]{1,0:T(8,128)(2,1)S(1)} %get-tuple-element.81), channel_id=1, source_target_pairs={{0,2},{1,3},{2,0},{3,1},{4,6},{5,7},{6,4},{7,5},{8,10},{9,11},{10,... | collective-permute-start | bytes 393224 | tf_op jit(solution)/shard_map/ppermute | solution.py:577
  16.9 1.7 %collective-permute-done.3.refs_0_ = bf16[128,256]{1,0:T(8,128)(2,1)S(1)} collective-permute-done((bf16[128,256]{1,0:T(8,128)(2,1)S(1)}, bf16[128,256]{1,0:T(8,128)(2,1)S(1)}, u32[]{:S(2)}, u32[]{:S(2)}) %collective-permute-start.3) | collective-permute-done | bytes 65568 | tf_op jit(solution)/shard_map/ppermute | solution.py:577
  18.7 1.4 %collective-permute-done.4.refs_1_ = bf16[128,256]{1,0:T(8,128)(2,1)S(1)} collective-permute-done((bf16[128,256]{1,0:T(8,128)(2,1)S(1)}, bf16[128,256]{1,0:T(8,128)(2,1)S(1)}, u32[]{:S(2)}, u32[]{:S(2)}) %collective-permute-start.4) | collective-permute-done | bytes 65568 | tf_op jit(solution)/shard_map/ppermute | solution.py:577
  20.0 1.0 %shard_map.79 = (bf16[128,512]{1,0:T(8,128)(2,1)S(1)}, bf16[128,512]{1,0:T(8,128)(2,1)S(1)}, f32[128,256]{1,0:T(8,128)S(1)}, f32[128,256]{1,0:T(8,128)S(1)}, bf16[256,256]{1,0:T(8,128)(2,1)S(1)}) custom-call(s32[1]{0:T(128)} %bitcast.place, f32[256,256]{1,0:T(8,128)S(1)} %get-tuple-element.48.bias, bf16[128,5120]{1,0:T(8,128)(2,1)S(1)} %get-tuple-element.53.own_all, ...), custom_call_target="tpu_custom_call" | custom-call | flops 671088640 | tf_op jit(solution)/shard_map/pallas_call | solution.py:536
  21.1 2.5 %collective-permute-start.5 = (bf16[256,256]{1,0:T(8,128)(2,1)S(1)}, bf16[256,256]{1,0:T(8,128)(2,1)S(1)}, u32[]{:S(2)}, u32[]{:S(2)}) collective-permute-start(bf16[256,256]{1,0:T(8,128)(2,1)S(1)} %get-tuple-element.57), channel_id=1, source_target_pairs={{0,2},{1,3},{2,0},{3,1},{4,6},{5,7},{6,4},{7,5},{8,10},{9,11},{10,... | collective-permute-start | bytes 393224 | tf_op jit(solution)/shard_map/ppermute | solution.py:577
  23.6 1.0 %shard_map.81 = (bf16[128,512]{1,0:T(8,128)(2,1)S(1)}, bf16[128,512]{1,0:T(8,128)(2,1)S(1)}, f32[128,256]{1,0:T(8,128)S(1)}, f32[128,256]{1,0:T(8,128)S(1)}, bf1...) custom-call(s32[1]{0:T(128)} %bitcast.place, ...), custom_call_target="tpu_custom_call" | custom-call | flops 671088640 | tf_op jit(solution)/shard_map/pallas_call | solution.py:536
  24.8 0.5 %collective-permute-start.14 = (bf16[128,512]{1,0:T(8,128)(2,1)S(1)}, bf16[128,512]{1,0:T(8,128)(2,1)S(1)}, u32[]{:S(2)}, u32[]{:S(2)}) collective-permute-start(bf16[128,512]{1,0:T(8,128)(2,1)S(1)} %get-tuple-element.75), channel_id=1, source_target_pairs={{0,1},{1,0},{2,3},{3,2},{4,5},{5,4},{6,7},{7,6},{8,9},{9,8},{10,11... | collective-permute-start | bytes 393224 | tf_op jit(solution)/shard_map/ppermute | solution.py:577
  25.3 0.4 %collective-permute-start.11 = (bf16[128,512]{1,0:T(8,128)(2,1)S(1)}, bf16[128,512]{1,0:T(8,128)(2,1)S(1)}, u32[]{:S(2)}, u32[]{:S(2)}) collective-permute-start(bf16[128,512]{1,0:T(8,128)(2,1)S(1)} %get-tuple-element.71), channel_id=1, source_target_pairs={{0,1},{1,0},{2,3},{3,2},{4,5},{5,4},{6,7},{7,6},{8,9},{9,8},{10,11... | collective-permute-start | bytes 393224 | tf_op jit(solution)/shard_map/ppermute | solution.py:577
  25.8 1.6 %collective-permute-done.5.refs_1_.refs_2_ = bf16[256,256]{1,0:T(8,128)(2,1)S(1)} collective-permute-done((bf16[256,256]{1,0:T(8,128)(2,1)S(1)}, bf16[256,256]{1,0:T(8,128)(2,1)S(1)}, u32[]{:S(2)}, u32[]{:S(2)}) %collective-permute-start.5) | collective-permute-done | bytes 131104 | tf_op jit(solution)/shard_map/ppermute | solution.py:577
  27.4 1.9 %collective-permute-start.10 = (bf16[128,256]{1,0:T(8,128)(2,1)S(1)}, bf16[128,256]{1,0:T(8,128)(2,1)S(1)}, u32[]{:S(2)}, u32[]{:S(2)}) collective-permute-start(bf16[128,256]{1,0:T(8,128)(2,1)S(1)} %get-tuple-element.69), channel_id=1, source_target_pairs={{0,3},{1,2},{2,1},{3,0},{4,7},{5,6},{6,5},{7,4},{8,11},{9,10},{10,... | collective-permute-start | bytes 196616 | tf_op jit(solution)/shard_map/ppermute | solution.py:577
  29.6 1.2 %shard_map.85 = (bf16[128,4096]{1,0:T(8,128)(2,1)}, bf16[128,1024]{1,0:T(8,128)(2,1)}, bf16[128,1024]{1,0:T(8,128)(2,1)}) custom-call(s32[1]{0:T(128)} %bitcast.place, bf16[128,512]{1,0:T(8,128)(2,1)S(1)} %get-tuple-element.70.refs_0_, bf16[128,512]{1,0:T(8,128)(2,1)S(1)} %collective-permute-done.11.refs_1_, bf16[128,512]{1,0:T(8,128)(2,1)S(1)} %get-tuple-element.74.refs_2_, ...), custom_call_target="tpu_custom_call" | custom-call | tf_op jit(solution)/shard_map/pallas_call | solution.py:536
  30.8 1.0 %collective-permute-done.10.refs_6_ = bf16[128,256]{1,0:T(8,128)(2,1)S(1)} collective-permute-done((bf16[128,256]{1,0:T(8,128)(2,1)S(1)}, bf16[128,256]{1,0:T(8,128)(2,1)S(1)}, u32[]{:S(2)}, u32[]{:S(2)}) %collective-permute-start.10) | collective-permute-done | bytes 65568 | tf_op jit(solution)/shard_map/ppermute | solution.py:577
  31.8 1.8 %collective-permute-done.8.refs_4_ = bf16[128,256]{1,0:T(8,128)(2,1)S(1)} collective-permute-done((bf16[128,256]{1,0:T(8,128)(2,1)S(1)}, bf16[128,256]{1,0:T(8,128)(2,1)S(1)}, u32[]{:S(2)}, u32[]{:S(2)}) %collective-permute-start.8) | collective-permute-done | bytes 65568 | tf_op jit(solution)/shard_map/ppermute | solution.py:577
  33.6 0.8 %shard_map.86 = (bf16[128,4096]{1,0:T(8,128)(2,1)}, bf16[128,1024]{1,0:T(8,128)(2,1)}, bf16[128,1024]{1,0:T(8,128)(2,1)}) custom-call(s32[1]{0:T(128)} %bitcast.place, bf16[128,256]{1,0:T(8,128)(2,1)S(1)} %collective-permute-done.6.refs_0_, f32[128,256]{1,0:T(8,128)S(1)} %get-tuple-element.58.refs_1_, ...), custom_call_target="tpu_custom_call", output_to_operand_aliasing={{0}: (8, {}), {1}: (9, {}), {2}: (10, {})} | custom-call | tf_op jit(solution)/shard_map/pallas_call | solution.py:536
  (23 shorter events, 0.9 us)
Async XLA Ops:
  2.5 7.0 %collective-permute-start = (bf16[128,5120]{1,0:T(8,128)(2,1)S(1)}, bf16[128,5120]{1,0:T(8,128)(2,1)S(1)}, u32[]{:S(2)}, u32[]{:S(2)}) collective-permute-start(bf16[128,5120]{1,0:T(8,128)(2,1)S(1)} %get-tuple-element.50), channel_id=1, source_target_pairs={{0,1},{1,0},{2,3},{3,2},{4,5},{5,4},{6,7},{7,6},{8,9},{9,8},{10,11... | collective-permute-start | bytes 3932168 | tf_op jit(solution)/shard_map/ppermute | solution.py:577
  3.1 5.0 %collective-permute-start.1 = (bf16[128,256]{1,0:T(8,128)(2,1)S(1)}, bf16[128,256]{1,0:T(8,128)(2,1)S(1)}, u32[]{:S(2)}, u32[]{:S(2)}) collective-permute-start(bf16[128,256]{1,0:T(8,128)(2,1)S(1)} %get-tuple-element.51), channel_id=1, source_target_pairs={{0,2},{1,3},{2,0},{3,1},{4,6},{5,7},{6,4},{7,5},{8,10},{9,11},{10,... | collective-permute-start | bytes 196616 | tf_op jit(solution)/shard_map/ppermute | solution.py:577
  5.4 4.1 %collective-permute-start.2 = (bf16[128,256]{1,0:T(8,128)(2,1)S(1)}, bf16[128,256]{1,0:T(8,128)(2,1)S(1)}, u32[]{:S(2)}, u32[]{:S(2)}) collective-permute-start(bf16[128,256]{1,0:T(8,128)(2,1)S(1)} %get-tuple-element.52), channel_id=1, source_target_pairs={{0,3},{1,2},{2,1},{3,0},{4,7},{5,6},{6,5},{7,4},{8,11},{9,10},{10,... | collective-permute-start | bytes 196616 | tf_op jit(solution)/shard_map/ppermute | solution.py:577
  5.5 9.2 %collective-permute-start.12 = (bf16[128,256]{1,0:T(8,128)(2,1)S(1)}, bf16[128,256]{1,0:T(8,128)(2,1)S(1)}, u32[]{:S(2)}, u32[]{:S(2)}) collective-permute-start(bf16[128,256]{1,0:T(8,128)(2,1)S(1)} %get-tuple-element.72), channel_id=1, source_target_pairs={{0,2},{1,3},{2,0},{3,1},{4,6},{5,7},{6,4},{7,5},{8,10},{9,11},{10,... | collective-permute-start | bytes 196616 | tf_op jit(solution)/shard_map/ppermute | solution.py:577
  7.2 7.4 %collective-permute-start.13 = (bf16[128,256]{1,0:T(8,128)(2,1)S(1)}, bf16[128,256]{1,0:T(8,128)(2,1)S(1)}, u32[]{:S(2)}, u32[]{:S(2)}) collective-permute-start(bf16[128,256]{1,0:T(8,128)(2,1)S(1)} %get-tuple-element.73), channel_id=1, source_target_pairs={{0,3},{1,2},{2,1},{3,0},{4,7},{5,6},{6,5},{7,4},{8,11},{9,10},{10,... | collective-permute-start | bytes 196616 | tf_op jit(solution)/shard_map/ppermute | solution.py:577
  10.8 12.8 %collective-permute-start.7 = (bf16[256,256]{1,0:T(8,128)(2,1)S(1)}, bf16[256,256]{1,0:T(8,128)(2,1)S(1)}, u32[]{:S(2)}, u32[]{:S(2)}) collective-permute-start(bf16[256,256]{1,0:T(8,128)(2,1)S(1)} %get-tuple-element.59), channel_id=1, source_target_pairs={{0,2},{1,3},{2,0},{3,1},{4,6},{5,7},{6,4},{7,5},{8,10},{9,11},{10,... | collective-permute-start | bytes 393224 | tf_op jit(solution)/shard_map/ppermute | solution.py:577
  12.7 6.0 %collective-permute-start.3 = (bf16[128,256]{1,0:T(8,128)(2,1)S(1)}, bf16[128,256]{1,0:T(8,128)(2,1)S(1)}, u32[]{:S(2)}, u32[]{:S(2)}) collective-permute-start(bf16[128,256]{1,0:T(8,128)(2,1)S(1)} %get-tuple-element.54), channel_id=1, source_target_pairs={{0,2},{1,3},{2,0},{3,1},{4,6},{5,7},{6,4},{7,5},{8,10},{9,11},{10,... | collective-permute-start | bytes 196616 | tf_op jit(solution)/shard_map/ppermute | solution.py:577
  12.9 7.1 %collective-permute-start.4 = (bf16[128,256]{1,0:T(8,128)(2,1)S(1)}, bf16[128,256]{1,0:T(8,128)(2,1)S(1)}, u32[]{:S(2)}, u32[]{:S(2)}) collective-permute-start(bf16[128,256]{1,0:T(8,128)(2,1)S(1)} %get-tuple-element.55), channel_id=1, source_target_pairs={{0,3},{1,2},{2,1},{3,0},{4,7},{5,6},{6,5},{7,4},{8,11},{9,10},{10,... | collective-permute-start | bytes 196616 | tf_op jit(solution)/shard_map/ppermute | solution.py:577
  15.7 9.7 %collective-permute-start.16 = (bf16[256,256]{1,0:T(8,128)(2,1)S(1)}, bf16[256,256]{1,0:T(8,128)(2,1)S(1)}, u32[]{:S(2)}, u32[]{:S(2)}) collective-permute-start(bf16[256,256]{1,0:T(8,128)(2,1)S(1)} %get-tuple-element.81), channel_id=1, source_target_pairs={{0,2},{1,3},{2,0},{3,1},{4,6},{5,7},{6,4},{7,5},{8,10},{9,11},{10,... | collective-permute-start | bytes 393224 | tf_op jit(solution)/shard_map/ppermute | solution.py:577
  21.1 6.3 %collective-permute-start.5 = (bf16[256,256]{1,0:T(8,128)(2,1)S(1)}, bf16[256,256]{1,0:T(8,128)(2,1)S(1)}, u32[]{:S(2)}, u32[]{:S(2)}) collective-permute-start(bf16[256,256]{1,0:T(8,128)(2,1)S(1)} %get-tuple-element.57), channel_id=1, source_target_pairs={{0,2},{1,3},{2,0},{3,1},{4,6},{5,7},{6,4},{7,5},{8,10},{9,11},{10,... | collective-permute-start | bytes 393224 | tf_op jit(solution)/shard_map/ppermute | solution.py:577
  24.7 4.9 %collective-permute-start.9 = (bf16[128,768]{1,0:T(8,128)(2,1)S(1)}, bf16[128,768]{1,0:T(8,128)(2,1)S(1)}, u32[]{:S(2)}, u32[]{:S(2)}) collective-permute-start(bf16[128,768]{1,0:T(8,128)(2,1)S(1)} %get-tuple-element.68), channel_id=1, source_target_pairs={{0,1},{1,0},{2,3},{3,2},{4,5},{5,4},{6,7},{7,6},{8,9},{9,8},{10,11... | collective-permute-start | bytes 589832 | tf_op jit(solution)/shard_map/ppermute | solution.py:577
  24.8 2.6 %collective-permute-start.14 = (bf16[128,512]{1,0:T(8,128)(2,1)S(1)}, bf16[128,512]{1,0:T(8,128)(2,1)S(1)}, u32[]{:S(2)}, u32[]{:S(2)}) collective-permute-start(bf16[128,512]{1,0:T(8,128)(2,1)S(1)} %get-tuple-element.75), channel_id=1, source_target_pairs={{0,1},{1,0},{2,3},{3,2},{4,5},{5,4},{6,7},{7,6},{8,9},{9,8},{10,11... | collective-permute-start | bytes 393224 | tf_op jit(solution)/shard_map/ppermute | solution.py:577
  25.3 4.1 %collective-permute-start.15 = (bf16[128,512]{1,0:T(8,128)(2,1)S(1)}, bf16[128,512]{1,0:T(8,128)(2,1)S(1)}, u32[]{:S(2)}, u32[]{:S(2)}) collective-permute-start(bf16[128,512]{1,0:T(8,128)(2,1)S(1)} %get-tuple-element.77), channel_id=1, source_target_pairs={{0,1},{1,0},{2,3},{3,2},{4,5},{5,4},{6,7},{7,6},{8,9},{9,8},{10,11... | collective-permute-start | bytes 393224 | tf_op jit(solution)/shard_map/ppermute | solution.py:577
  25.3 4.3 %collective-permute-start.11 = (bf16[128,512]{1,0:T(8,128)(2,1)S(1)}, bf16[128,512]{1,0:T(8,128)(2,1)S(1)}, u32[]{:S(2)}, u32[]{:S(2)}) collective-permute-start(bf16[128,512]{1,0:T(8,128)(2,1)S(1)} %get-tuple-element.71), channel_id=1, source_target_pairs={{0,1},{1,0},{2,3},{3,2},{4,5},{5,4},{6,7},{7,6},{8,9},{9,8},{10,11... | collective-permute-start | bytes 393224 | tf_op jit(solution)/shard_map/ppermute | solution.py:577
  27.4 2.3 %collective-permute-start.17 = (bf16[128,512]{1,0:T(8,128)(2,1)S(1)}, bf16[128,512]{1,0:T(8,128)(2,1)S(1)}, u32[]{:S(2)}, u32[]{:S(2)}) collective-permute-start(bf16[128,512]{1,0:T(8,128)(2,1)S(1)} %shard_map.84), channel_id=1, source_target_pairs={{0,1},{1,0},{2,3},{3,2},{4,5},{5,4},{6,7},{7,6},{8,9},{9,8},{10,11... | collective-permute-start | bytes 393224 | tf_op jit(solution)/shard_map/ppermute | solution.py:577
  27.4 4.4 %collective-permute-start.10 = (bf16[128,256]{1,0:T(8,128)(2,1)S(1)}, bf16[128,256]{1,0:T(8,128)(2,1)S(1)}, u32[]{:S(2)}, u32[]{:S(2)}) collective-permute-start(bf16[128,256]{1,0:T(8,128)(2,1)S(1)} %get-tuple-element.69), channel_id=1, source_target_pairs={{0,3},{1,2},{2,1},{3,0},{4,7},{5,6},{6,5},{7,4},{8,11},{9,10},{10,... | collective-permute-start | bytes 196616 | tf_op jit(solution)/shard_map/ppermute | solution.py:577
  29.3 4.3 %collective-permute-start.8 = (bf16[128,256]{1,0:T(8,128)(2,1)S(1)}, bf16[128,256]{1,0:T(8,128)(2,1)S(1)}, u32[]{:S(2)}, u32[]{:S(2)}) collective-permute-start(bf16[128,256]{1,0:T(8,128)(2,1)S(1)} %get-tuple-element.67), channel_id=1, source_target_pairs={{0,2},{1,3},{2,0},{3,1},{4,6},{5,7},{6,4},{7,5},{8,10},{9,11},{10,... | collective-permute-start | bytes 196616 | tf_op jit(solution)/shard_map/ppermute | solution.py:577
  29.6 4.0 %collective-permute-start.6 = (bf16[128,256]{1,0:T(8,128)(2,1)S(1)}, bf16[128,256]{1,0:T(8,128)(2,1)S(1)}, u32[]{:S(2)}, u32[]{:S(2)}) collective-permute-start(bf16[128,256]{1,0:T(8,128)(2,1)S(1)} %shard_map.80), channel_id=1, source_target_pairs={{0,1},{1,0},{2,3},{3,2},{4,5},{5,4},{6,7},{7,6},{8,9},{9,8},{10,11... | collective-permute-start | bytes 196616 | tf_op jit(solution)/shard_map/ppermute | solution.py:577
